TPU v7x, 768 devices: a whole 4x8x12 slice. The times are simulated.
768 devices in a mesh: lat: 96 (over y, z_hi, x), lon: 8 (over z_lo, core).
Axes of the slice: x: 4, y: 8, z: 12 (z_hi: 3, z_lo: 4; z = z_hi * 4 + z_lo), core: 2. Of those that a mesh axis runs over, the one named last changes fastest.
Arguments:
- right_side: float32 [1536, 5120], P('lat', 'lon'), may hold values from -34 to 34
- first_guess: float32 [1536, 5120], P('lat', 'lon'), may hold values from -3 to 3
- cell_mask: int32 [1536, 5120], P('lat', 'lon'), may hold values 0 or 1
- cond_east: float32 [1536, 5120], P('lat', 'lon'), may hold values from 0.5 to 2
- cond_north: float32 [1536, 5120], P('lat', 'lon'), may hold values from 0.5 to 2
- surface: float32 [1536, 5120], P('lat', 'lon'), may hold values from 0.02 to 0.5
- recycled: float32 [16, 1536, 5120], P(None, 'lat', 'lon'), may hold values from -0.0006418624 to 0.0006418624
Outputs:
- solution: float32 [1536, 5120], P('lat', 'lon')
- residual: float32 [1536, 5120], P('lat', 'lon')
All inputs are finite; a program needn't handle non-finite values. No bound on the sum of `cell_mask` on one device may be relied on, other than what follows from the above.
Results may differ from a plain program's by a relative error of at most 0.0003.
Values sent between devices are 32-bit elements; how exact they have to be, the bound alone decides.
A program may use at most 32 MiB of HBM per device.

v0:
```python
import functools

import jax
import jax.numpy as jnp
from jax import lax
from jax.sharding import Mesh
from jax.sharding import PartitionSpec as P

ITERS = 3
LAT = ("lat_0", "lat_1", "lat_2")
LAT_LON = ("lat_0", "lat_1", "lat_2", "lon_0", "lon_1")
LON = ("lon_0", "lon_1")


PRECISE = lax.Precision.HIGHEST


def with_halo(x, sides, width):
    edges = {}
    for axis, dim in sides:
        count, length = (lax.axis_size(axis), x.shape[dim])
        up = [(i, (i + 1) % count) for i in range(count)]
        last = lax.slice_in_dim(x, length - width, length, axis=dim)
        leading = lax.slice_in_dim(x, 0, width, axis=dim)
        edges[dim] = (
            lax.ppermute(last, axis, up),
            lax.ppermute(leading, axis, [(b, a) for a, b in up]),
        )
    done = []
    for _, dim in sides:
        low, high = edges[dim]
        around = [(width, width) if d in done else (0, 0) for d in range(x.ndim)]
        x = jnp.concatenate([jnp.pad(low, around), x, jnp.pad(high, around)], axis=dim)
        done.append(dim)
    return x


def one_axis_at_a_time(x, axes):
    return functools.reduce(lax.psum, axes, x)


def close_poles(padded):
    row_index = lax.axis_index(LAT)
    last_row = lax.axis_size(LAT) - 1
    keep_south = (row_index > 0).astype(jnp.float32)
    keep_north = (row_index < last_row).astype(jnp.float32)
    return jnp.concatenate(
        [padded[..., :1, :] * keep_south, padded[..., 1:-1, :], padded[..., -1:, :] * keep_north],
        axis=-2,
    )


def faces(side, surface):
    wet_pad = side[0]
    east_pad = side[1]
    north_pad = side[2]
    wet_cells = wet_pad[1:-1, 1:-1]
    k_east = east_pad[1:-1, 1:-1] * wet_pad[1:-1, 2:]
    k_west = east_pad[1:-1, :-2] * wet_cells
    k_north = north_pad[1:-1, 1:-1] * wet_pad[2:, 1:-1]
    k_south = north_pad[:-2, 1:-1] * wet_cells
    centre = surface * wet_cells + k_east + k_west + k_north + k_south + (1.0 - wet_cells)
    return (centre, k_east, k_west, k_north, k_south)


def operate_padded(padded, coeffs):
    centre, k_east, k_west, k_north, k_south = coeffs
    inner = padded[..., 1:-1, 1:-1]
    to_east = padded[..., 1:-1, 2:]
    to_west = padded[..., 1:-1, :-2]
    to_north = padded[..., 2:, 1:-1]
    to_south = padded[..., :-2, 1:-1]
    return centre * inner - (
        k_east * to_east + k_west * to_west + k_north * to_north + k_south * to_south
    )


def residual_image(residual, coeffs):
    padded = with_halo(residual, ((LAT, 0), (LON, 1)), 1)
    return operate_padded(padded, coeffs)


def solve_small(factor, target):
    return jax.scipy.linalg.cho_solve((factor, True), target)


def shards(right_side, first_guess, cell_mask, cond_east, cond_north, surface, recycled):
    wet_cells = cell_mask.astype(jnp.float32)
    local_side = jnp.stack([wet_cells, cond_east * wet_cells, cond_north * wet_cells, first_guess])
    padded_all = with_halo(jnp.concatenate([local_side, recycled], axis=0), ((LAT, 1), (LON, 2)), 1)
    side_pad = close_poles(padded_all[:3])
    guess_pad = padded_all[3]
    basis_pad = padded_all[4:]
    coeffs = faces(side_pad, surface)
    basis_image = operate_padded(basis_pad, coeffs)
    start_res = right_side - operate_padded(guess_pad, coeffs)
    gram_local = jnp.einsum("kyx,lyx->kl", recycled, basis_image, precision=PRECISE)
    start_local = jnp.einsum("kyx,yx->k", recycled, start_res, precision=PRECISE)
    gram, start = (
        one_axis_at_a_time(gram_local, LAT_LON),
        one_axis_at_a_time(start_local, LAT_LON),
    )
    factor = jnp.linalg.cholesky(0.5 * (gram + gram.T))
    coarse = solve_small(factor, start)
    solution = first_guess + jnp.einsum("kyx,k->yx", recycled, coarse, precision=PRECISE)
    residual = start_res - jnp.einsum("kyx,k->yx", basis_image, coarse, precision=PRECISE)
    direction = residual
    dir_image = residual
    curv = jnp.float32(1.0)
    prev_norm = jnp.float32(1.0)
    for turn_index in range(ITERS):
        image_res = residual_image(residual, coeffs)
        defl_local = jnp.einsum("kyx,yx->k", recycled, image_res, precision=PRECISE)
        res_norm, res_image, defl = (
            one_axis_at_a_time(jnp.sum(residual * residual), LAT_LON),
            one_axis_at_a_time(jnp.sum(residual * image_res), LAT_LON),
            one_axis_at_a_time(defl_local, LAT_LON),
        )
        coef = solve_small(factor, defl)
        along_basis = jnp.einsum("kyx,k->yx", recycled, coef, precision=PRECISE)
        along_image = jnp.einsum("kyx,k->yx", basis_image, coef, precision=PRECISE)
        if turn_index == 0:
            direction = residual - along_basis
            dir_image = image_res - along_image
            curv = res_image - jnp.sum(coef * defl)
        else:
            ratio = res_norm / prev_norm
            direction = residual - along_basis + ratio * direction
            dir_image = image_res - along_image + ratio * dir_image
            curv = res_image - jnp.sum(coef * defl) - ratio * ratio * curv
        step_len = res_norm / curv
        solution = solution + step_len * direction
        residual = residual - step_len * dir_image
        prev_norm = res_norm
    return (solution, residual)


def solution(mesh):
    finer = Mesh(mesh.devices.reshape(8, 3, 4, 4, 2), ("lat_0", "lat_1", "lat_2", "lon_0", "lon_1"))
    in_specs = (
        P(LAT, LON),
        P(LAT, LON),
        P(LAT, LON),
        P(LAT, LON),
        P(LAT, LON),
        P(LAT, LON),
        P(None, LAT, LON),
    )
    out_specs = (P(LAT, LON), P(LAT, LON))
    return jax.shard_map(
        shards, mesh=finer, in_specs=in_specs, out_specs=out_specs, check_vma=False
    )
```

profile of v0, /device:TPU:1, one launch (start us, length us, event | category | flops | bytes accessed | tf_op | source)
XLA Modules:
  0.0 331.6 jit_solution(14440115993009593359)
XLA Ops:
  4.3 20.2 %collective-permute-start.2 = (f32[20,1,640]{2,1,0:T(1,128)S(1)}, f32[20,1,640]{2,1,0:T(1,128)S(1)}, u32[]{:S(2)}, u32[]{:S(2)}) collective-permute-start(f32[20,1,640]{2,1,0:T(1,128)S(1)} %get-tuple-element.78), channel_id=1, source_target_pairs={{8,0},{16,8},{24,16},{32,24},{40,32},{48,40},{56,48},{64,56},{72,6... | collective-permute-start | bytes 153608 | tf_op jit(solution)/shard_map/ppermute | solution.py:27
  45.2 11.2 %all-reduce.11 = (f32[16,16]{0,1:T(8,128)S(1)}, f32[16]{0:T(128)S(1)}) all-reduce(f32[16,16]{0,1:T(8,128)S(1)} %convolution_bitcast_fusion, f32[16]{0:T(128)S(1)} %convolution_bitcast_fusion.9), channel_id=1, replica_groups=mesh['lat_0'=8,'lat_1'=3,'lat_2'=4,'lon_0'=4,'lon_1'=2] {'lat_0'}, use_global_device_ids=true, to_apply=%region_0.1 | all-reduce | flops 272 | bytes 2176 | tf_op jit(solution)/shard_map/psum | solution.py:39
  56.4 7.8 %all-reduce.23 = (f32[16,16]{0,1:T(8,128)S(1)}, f32[16]{0:T(128)S(1)}) all-reduce(f32[16,16]{0,1:T(8,128)S(1)} %get-tuple-element.18, f32[16]{0:T(128)S(1)} %get-tuple-element.19), channel_id=1, replica_groups=mesh['lat_0'=8,'lat_1'=3,'lat_2'=4,'lon_0'=4,'lon_1'=2] {'lat_1'}, use_global_device_ids=true, to_apply=%region_1.2 | all-reduce | flops 272 | bytes 2176 | tf_op jit(solution)/shard_map/psum | solution.py:39
  64.2 9.5 %all-reduce.19 = (f32[16,16]{0,1:T(8,128)S(1)}, f32[16]{0:T(128)S(1)}) all-reduce(f32[16,16]{0,1:T(8,128)S(1)} %get-tuple-element.51, f32[16]{0:T(128)S(1)} %get-tuple-element.52), channel_id=1, replica_groups=mesh['lat_0'=8,'lat_1'=3,'lat_2'=4,'lon_0'=4,'lon_1'=2] {'lat_2'}, use_global_device_ids=true, to_apply=%region_2.3 | all-reduce | flops 272 | bytes 2176 | tf_op jit(solution)/shard_map/psum | solution.py:39
  73.7 9.9 %all-reduce.15 = (f32[16,16]{0,1:T(8,128)S(1)}, f32[16]{0:T(128)S(1)}) all-reduce(f32[16,16]{0,1:T(8,128)S(1)} %get-tuple-element.40, f32[16]{0:T(128)S(1)} %get-tuple-element.41), channel_id=1, replica_groups=mesh['lat_0'=8,'lat_1'=3,'lat_2'=4,'lon_0'=4,'lon_1'=2] {'lon_0'}, use_global_device_ids=true, to_apply=%region_3.4 | all-reduce | flops 272 | bytes 2176 | tf_op jit(solution)/shard_map/psum | solution.py:39
  83.6 12.2 %all-reduce.27 = (f32[16,16]{0,1:T(8,128)S(1)}, f32[16]{0:T(128)S(1)}) all-reduce(f32[16,16]{0,1:T(8,128)S(1)} %get-tuple-element.29, f32[16]{0:T(128)S(1)} %get-tuple-element.30), channel_id=1, replica_groups=mesh['lat_0'=8,'lat_1'=3,'lat_2'=4,'lon_0'=4,'lon_1'=2] {'lon_1'}, use_global_device_ids=true, to_apply=%region_4.5 | all-reduce | flops 272 | bytes 2176 | tf_op jit(solution)/shard_map/psum | solution.py:39
  103.5 11.5 %collective-permute-start.5 = (f32[1,640]{1,0:T(1,128)S(1)}, f32[1,640]{1,0:T(1,128)S(1)}, u32[]{:S(2)}, u32[]{:S(2)}) collective-permute-start(f32[1,640]{1,0:T(1,128)S(1)} %get-tuple-element.96), channel_id=1, source_target_pairs={{8,0},{16,8},{24,16},{32,24},{40,32},{48,40},{56,48},{64,56},{72,6... | collective-permute-start | bytes 7688 | tf_op jit(solution)/shard_map/ppermute | solution.py:27
  125.5 11.3 %all-reduce.10 = (f32[]{:T(128)}, f32[]{:T(128)}, f32[16]{0:T(128)S(1)}) all-reduce(f32[]{:T(128)} %get-tuple-element.8, f32[]{:T(128)} %get-tuple-element.7, f32[16]{0:T(128)S(1)} %convolution_bitcast_fusion.6), channel_id=1, replica_groups=mesh['lat_0'=8,'lat_1'=3,'lat_2'=4,'lon_0'=4,'lon_1'=2] {'lat_0'}, use_global_device_ids=true, to_apply=%region_13.15 | all-reduce | flops 18 | bytes 144 | tf_op jit(solution)/shard_map/psum | solution.py:39
  136.8 8.3 %all-reduce.22 = (f32[]{:T(128)}, f32[]{:T(128)}, f32[16]{0:T(128)S(1)}) all-reduce(f32[]{:T(128)} %get-tuple-element.15, f32[]{:T(128)} %get-tuple-element.16, f32[16]{0:T(128)S(1)} %get-tuple-element.17), channel_id=1, replica_groups=mesh['lat_0'=8,'lat_1'=3,'lat_2'=4,'lon_0'=4,'lon_1'=2] {'lat_1'}, use_global_device_ids=true, to_apply=%region_14.16 | all-reduce | flops 18 | bytes 144 | tf_op jit(solution)/shard_map/psum | solution.py:39
  145.1 6.9 %all-reduce.18 = (f32[]{:T(128)}, f32[]{:T(128)}, f32[16]{0:T(128)S(1)}) all-reduce(f32[]{:T(128)} %get-tuple-element.48, f32[]{:T(128)} %get-tuple-element.49, f32[16]{0:T(128)S(1)} %get-tuple-element.50), channel_id=1, replica_groups=mesh['lat_0'=8,'lat_1'=3,'lat_2'=4,'lon_0'=4,'lon_1'=2] {'lat_2'}, use_global_device_ids=true, to_apply=%region_15.17 | all-reduce | flops 18 | bytes 144 | tf_op jit(solution)/shard_map/psum | solution.py:39
  152.0 11.0 %all-reduce.14 = (f32[]{:T(128)}, f32[]{:T(128)}, f32[16]{0:T(128)S(1)}) all-reduce(f32[]{:T(128)} %get-tuple-element.37, f32[]{:T(128)} %get-tuple-element.38, f32[16]{0:T(128)S(1)} %get-tuple-element.39), channel_id=1, replica_groups=mesh['lat_0'=8,'lat_1'=3,'lat_2'=4,'lon_0'=4,'lon_1'=2] {'lon_0'}, use_global_device_ids=true, to_apply=%region_16.18 | all-reduce | flops 18 | bytes 144 | tf_op jit(solution)/shard_map/psum | solution.py:39
  162.9 10.3 %all-reduce.26 = (f32[]{:T(128)}, f32[]{:T(128)}, f32[16]{0:T(128)S(1)}) all-reduce(f32[]{:T(128)} %get-tuple-element.26, f32[]{:T(128)} %get-tuple-element.27, f32[16]{0:T(128)S(1)} %get-tuple-element.28), channel_id=1, replica_groups=mesh['lat_0'=8,'lat_1'=3,'lat_2'=4,'lon_0'=4,'lon_1'=2] {'lon_1'}, use_global_device_ids=true, to_apply=%region_17.19 | all-reduce | flops 18 | bytes 144 | tf_op jit(solution)/shard_map/psum | solution.py:39
  179.4 11.5 %collective-permute-start.9 = (f32[1,640]{1,0:T(1,128)S(1)}, f32[1,640]{1,0:T(1,128)S(1)}, u32[]{:S(2)}, u32[]{:S(2)}) collective-permute-start(f32[1,640]{1,0:T(1,128)S(1)} %get-tuple-element.92), channel_id=1, source_target_pairs={{8,0},{16,8},{24,16},{32,24},{40,32},{48,40},{56,48},{64,56},{72,6... | collective-permute-start | bytes 7688 | tf_op jit(solution)/shard_map/ppermute | solution.py:27
  200.5 11.4 %all-reduce.9 = (f32[16]{0:T(128)S(1)}, f32[]{:T(128)}, f32[]{:T(128)}) all-reduce(f32[16]{0:T(128)S(1)} %convolution_bitcast_fusion.4, f32[]{:T(128)} %get-tuple-element.6, f32[]{:T(128)} %get-tuple-element.5), channel_id=1, replica_groups=mesh['lat_0'=8,'lat_1'=3,'lat_2'=4,'lon_0'=4,'lon_1'=2] {'lat_0'}, use_global_device_ids=true, to_apply=%region_42.44 | all-reduce | flops 18 | bytes 144 | tf_op jit(solution)/shard_map/psum | solution.py:39
  211.9 8.3 %all-reduce.21 = (f32[16]{0:T(128)S(1)}, f32[]{:T(128)}, f32[]{:T(128)}) all-reduce(f32[16]{0:T(128)S(1)} %get-tuple-element.12, f32[]{:T(128)} %get-tuple-element.13, f32[]{:T(128)} %get-tuple-element.14), channel_id=1, replica_groups=mesh['lat_0'=8,'lat_1'=3,'lat_2'=4,'lon_0'=4,'lon_1'=2] {'lat_1'}, use_global_device_ids=true, to_apply=%region_43.45 | all-reduce | flops 18 | bytes 144 | tf_op jit(solution)/shard_map/psum | solution.py:39
  220.2 7.8 %all-reduce.17 = (f32[16]{0:T(128)S(1)}, f32[]{:T(128)}, f32[]{:T(128)}) all-reduce(f32[16]{0:T(128)S(1)} %get-tuple-element.45, f32[]{:T(128)} %get-tuple-element.46, f32[]{:T(128)} %get-tuple-element.47), channel_id=1, replica_groups=mesh['lat_0'=8,'lat_1'=3,'lat_2'=4,'lon_0'=4,'lon_1'=2] {'lat_2'}, use_global_device_ids=true, to_apply=%region_44.46 | all-reduce | flops 18 | bytes 144 | tf_op jit(solution)/shard_map/psum | solution.py:39
  228.0 11.0 %all-reduce.13 = (f32[16]{0:T(128)S(1)}, f32[]{:T(128)}, f32[]{:T(128)}) all-reduce(f32[16]{0:T(128)S(1)} %get-tuple-element.34, f32[]{:T(128)} %get-tuple-element.35, f32[]{:T(128)} %get-tuple-element.36), channel_id=1, replica_groups=mesh['lat_0'=8,'lat_1'=3,'lat_2'=4,'lon_0'=4,'lon_1'=2] {'lon_0'}, use_global_device_ids=true, to_apply=%region_45.47 | all-reduce | flops 18 | bytes 144 | tf_op jit(solution)/shard_map/psum | solution.py:39
  239.0 9.4 %all-reduce.25 = (f32[16]{0:T(128)S(1)}, f32[]{:T(128)}, f32[]{:T(128)}) all-reduce(f32[16]{0:T(128)S(1)} %get-tuple-element.23, f32[]{:T(128)} %get-tuple-element.24, f32[]{:T(128)} %get-tuple-element.25), channel_id=1, replica_groups=mesh['lat_0'=8,'lat_1'=3,'lat_2'=4,'lon_0'=4,'lon_1'=2] {'lon_1'}, use_global_device_ids=true, to_apply=%region_46.48 | all-reduce | flops 18 | bytes 144 | tf_op jit(solution)/shard_map/psum | solution.py:39
  255.9 11.4 %collective-permute-start.13 = (f32[1,640]{1,0:T(1,128)S(1)}, f32[1,640]{1,0:T(1,128)S(1)}, u32[]{:S(2)}, u32[]{:S(2)}) collective-permute-start(f32[1,640]{1,0:T(1,128)S(1)} %get-tuple-element.88), channel_id=1, source_target_pairs={{8,0},{16,8},{24,16},{32,24},{40,32},{48,40},{56,48},{64,56},{72,6... | collective-permute-start | bytes 7688 | tf_op jit(solution)/shard_map/ppermute | solution.py:27
  277.9 11.3 %all-reduce.8 = (f32[16]{0:T(128)S(1)}, f32[]{:T(128)}, f32[]{:T(128)}) all-reduce(f32[16]{0:T(128)S(1)} %convolution_bitcast_fusion.2, f32[]{:T(128)} %get-tuple-element.4, f32[]{:T(128)} %get-tuple-element.3), channel_id=1, replica_groups=mesh['lat_0'=8,'lat_1'=3,'lat_2'=4,'lon_0'=4,'lon_1'=2] {'lat_0'}, use_global_device_ids=true, to_apply=%region_60.62 | all-reduce | flops 18 | bytes 144 | tf_op jit(solution)/shard_map/psum | solution.py:39
  289.2 8.3 %all-reduce.20 = (f32[16]{0:T(128)S(1)}, f32[]{:T(128)}, f32[]{:T(128)}) all-reduce(f32[16]{0:T(128)S(1)} %get-tuple-element.9, f32[]{:T(128)} %get-tuple-element.10, f32[]{:T(128)} %get-tuple-element.11), channel_id=1, replica_groups=mesh['lat_0'=8,'lat_1'=3,'lat_2'=4,'lon_0'=4,'lon_1'=2] {'lat_1'}, use_global_device_ids=true, to_apply=%region_61.63 | all-reduce | flops 18 | bytes 144 | tf_op jit(solution)/shard_map/psum | solution.py:39
  297.5 6.8 %all-reduce.16 = (f32[16]{0:T(128)S(1)}, f32[]{:T(128)}, f32[]{:T(128)}) all-reduce(f32[16]{0:T(128)S(1)} %get-tuple-element.42, f32[]{:T(128)} %get-tuple-element.43, f32[]{:T(128)} %get-tuple-element.44), channel_id=1, replica_groups=mesh['lat_0'=8,'lat_1'=3,'lat_2'=4,'lon_0'=4,'lon_1'=2] {'lat_2'}, use_global_device_ids=true, to_apply=%region_62.64 | all-reduce | flops 18 | bytes 144 | tf_op jit(solution)/shard_map/psum | solution.py:39
  304.3 11.0 %all-reduce.12 = (f32[16]{0:T(128)S(1)}, f32[]{:T(128)}, f32[]{:T(128)}) all-reduce(f32[16]{0:T(128)S(1)} %get-tuple-element.31, f32[]{:T(128)} %get-tuple-element.32, f32[]{:T(128)} %get-tuple-element.33), channel_id=1, replica_groups=mesh['lat_0'=8,'lat_1'=3,'lat_2'=4,'lon_0'=4,'lon_1'=2] {'lon_0'}, use_global_device_ids=true, to_apply=%region_63.65 | all-reduce | flops 18 | bytes 144 | tf_op jit(solution)/shard_map/psum | solution.py:39
  315.3 10.2 %all-reduce.24 = (f32[16]{0:T(128)S(1)}, f32[]{:T(128)}, f32[]{:T(128)}) all-reduce(f32[16]{0:T(128)S(1)} %get-tuple-element.20, f32[]{:T(128)} %get-tuple-element.21, f32[]{:T(128)} %get-tuple-element.22), channel_id=1, replica_groups=mesh['lat_0'=8,'lat_1'=3,'lat_2'=4,'lon_0'=4,'lon_1'=2] {'lon_1'}, use_global_device_ids=true, to_apply=%region_64.66 | all-reduce | flops 18 | bytes 144 | tf_op jit(solution)/shard_map/psum | solution.py:39
  (99 shorter events, 73.5 us)
Async XLA Ops:
  0.6 0.9 copy-start.1
  0.6 0.9 copy-start.5
  1.5 0.8 copy-start.6
  2.3 0.8 copy-start.2
  4.3 31.8 %collective-permute-start.2 = (f32[20,1,640]{2,1,0:T(1,128)S(1)}, f32[20,1,640]{2,1,0:T(1,128)S(1)}, u32[]{:S(2)}, u32[]{:S(2)}) collective-permute-start(f32[20,1,640]{2,1,0:T(1,128)S(1)} %get-tuple-element.78), channel_id=1, source_target_pairs={{8,0},{16,8},{24,16},{32,24},{40,32},{48,40},{56,48},{64,56},{72,6... | collective-permute-start | bytes 153608 | tf_op jit(solution)/shard_map/ppermute | solution.py:27
  24.5 16.3 %collective-permute-start.1 = (f32[20,1,640]{2,1,0:T(1,128)S(1)}, f32[20,1,640]{2,1,0:T(1,128)S(1)}, u32[]{:S(2)}, u32[]{:S(2)}) collective-permute-start(f32[20,1,640]{2,1,0:T(1,128)S(1)} %get-tuple-element.77), channel_id=1, source_target_pairs={{0,8},{8,16},{16,24},{24,32},{32,40},{40,48},{48,56},{56,64},{64,7... | collective-permute-start | bytes 153608 | tf_op jit(solution)/shard_map/ppermute | solution.py:26
  26.5 6.9 %collective-permute-start.3 = (f32[20,16,1]{2,1,0:T(8,128)S(1)}, f32[20,16,1]{2,1,0:T(8,128)S(1)}, u32[]{:S(2)}, u32[]{:S(2)}) collective-permute-start(f32[20,16,1]{2,1,0:T(8,128)S(1)} %get-tuple-element.80), channel_id=1, source_target_pairs={{1,0},{2,1},{3,2},{4,3},{5,4},{6,5},{7,6},{0,7},{9,8},{10,9},{11,1... | collective-permute-start | bytes 3848 | tf_op jit(solution)/shard_map/ppermute | solution.py:27
  29.4 6.6 %collective-permute-start = (f32[20,16,1]{2,1,0:T(8,128)S(1)}, f32[20,16,1]{2,1,0:T(8,128)S(1)}, u32[]{:S(2)}, u32[]{:S(2)}) collective-permute-start(f32[20,16,1]{2,1,0:T(8,128)S(1)} %get-tuple-element.79), channel_id=1, source_target_pairs={{0,1},{1,2},{2,3},{3,4},{4,5},{5,6},{6,7},{7,0},{8,9},{9,10},{10,1... | collective-permute-start | bytes 3848 | tf_op jit(solution)/shard_map/ppermute | solution.py:26
  41.1 0.8 copy-start.3
  41.1 0.8 copy-start.4
  41.2 1.1 copy-start
  101.5 22.2 %collective-permute-start.4 = (f32[1,640]{1,0:T(1,128)S(1)}, f32[1,640]{1,0:T(1,128)S(1)}, u32[]{:S(2)}, u32[]{:S(2)}) collective-permute-start(f32[1,640]{1,0:T(1,128)S(1)} %get-tuple-element.97), channel_id=1, source_target_pairs={{0,8},{8,16},{16,24},{24,32},{32,40},{40,48},{48,56},{56,64},{64,7... | collective-permute-start | bytes 7688 | tf_op jit(solution)/shard_map/ppermute | solution.py:26
  103.5 20.3 %collective-permute-start.5 = (f32[1,640]{1,0:T(1,128)S(1)}, f32[1,640]{1,0:T(1,128)S(1)}, u32[]{:S(2)}, u32[]{:S(2)}) collective-permute-start(f32[1,640]{1,0:T(1,128)S(1)} %get-tuple-element.96), channel_id=1, source_target_pairs={{8,0},{16,8},{24,16},{32,24},{40,32},{48,40},{56,48},{64,56},{72,6... | collective-permute-start | bytes 7688 | tf_op jit(solution)/shard_map/ppermute | solution.py:27
  115.0 5.7 %collective-permute-start.7 = (f32[16,1]{1,0:T(8,128)S(1)}, f32[16,1]{1,0:T(8,128)S(1)}, u32[]{:S(2)}, u32[]{:S(2)}) collective-permute-start(f32[16,1]{1,0:T(8,128)S(1)} %get-tuple-element.95), channel_id=1, source_target_pairs={{0,1},{1,2},{2,3},{3,4},{4,5},{5,6},{6,7},{7,0},{8,9},{9,10},{10,1... | collective-permute-start | bytes 200 | tf_op jit(solution)/shard_map/ppermute | solution.py:26
  118.8 5.0 %collective-permute-start.6 = (f32[16,1]{1,0:T(8,128)S(1)}, f32[16,1]{1,0:T(8,128)S(1)}, u32[]{:S(2)}, u32[]{:S(2)}) collective-permute-start(f32[16,1]{1,0:T(8,128)S(1)} %get-tuple-element.94), channel_id=1, source_target_pairs={{1,0},{2,1},{3,2},{4,3},{5,4},{6,5},{7,6},{0,7},{9,8},{10,9},{11,1... | collective-permute-start | bytes 200 | tf_op jit(solution)/shard_map/ppermute | solution.py:27
  177.5 21.4 %collective-permute-start.8 = (f32[1,640]{1,0:T(1,128)S(1)}, f32[1,640]{1,0:T(1,128)S(1)}, u32[]{:S(2)}, u32[]{:S(2)}) collective-permute-start(f32[1,640]{1,0:T(1,128)S(1)} %get-tuple-element.93), channel_id=1, source_target_pairs={{0,8},{8,16},{16,24},{24,32},{32,40},{40,48},{48,56},{56,64},{64,7... | collective-permute-start | bytes 7688 | tf_op jit(solution)/shard_map/ppermute | solution.py:26
  179.4 19.4 %collective-permute-start.9 = (f32[1,640]{1,0:T(1,128)S(1)}, f32[1,640]{1,0:T(1,128)S(1)}, u32[]{:S(2)}, u32[]{:S(2)}) collective-permute-start(f32[1,640]{1,0:T(1,128)S(1)} %get-tuple-element.92), channel_id=1, source_target_pairs={{8,0},{16,8},{24,16},{32,24},{40,32},{48,40},{56,48},{64,56},{72,6... | collective-permute-start | bytes 7688 | tf_op jit(solution)/shard_map/ppermute | solution.py:27
  191.0 4.8 %collective-permute-start.11 = (f32[16,1]{1,0:T(8,128)S(1)}, f32[16,1]{1,0:T(8,128)S(1)}, u32[]{:S(2)}, u32[]{:S(2)}) collective-permute-start(f32[16,1]{1,0:T(8,128)S(1)} %get-tuple-element.91), channel_id=1, source_target_pairs={{0,1},{1,2},{2,3},{3,4},{4,5},{5,6},{6,7},{7,0},{8,9},{9,10},{10,1... | collective-permute-start | bytes 200 | tf_op jit(solution)/shard_map/ppermute | solution.py:26
  193.9 5.0 %collective-permute-start.10 = (f32[16,1]{1,0:T(8,128)S(1)}, f32[16,1]{1,0:T(8,128)S(1)}, u32[]{:S(2)}, u32[]{:S(2)}) collective-permute-start(f32[16,1]{1,0:T(8,128)S(1)} %get-tuple-element.90), channel_id=1, source_target_pairs={{1,0},{2,1},{3,2},{4,3},{5,4},{6,5},{7,6},{0,7},{9,8},{10,9},{11,1... | collective-permute-start | bytes 200 | tf_op jit(solution)/shard_map/ppermute | solution.py:27
  253.9 22.3 %collective-permute-start.12 = (f32[1,640]{1,0:T(1,128)S(1)}, f32[1,640]{1,0:T(1,128)S(1)}, u32[]{:S(2)}, u32[]{:S(2)}) collective-permute-start(f32[1,640]{1,0:T(1,128)S(1)} %get-tuple-element.89), channel_id=1, source_target_pairs={{0,8},{8,16},{16,24},{24,32},{32,40},{40,48},{48,56},{56,64},{64,7... | collective-permute-start | bytes 7688 | tf_op jit(solution)/shard_map/ppermute | solution.py:26
  255.9 20.3 %collective-permute-start.13 = (f32[1,640]{1,0:T(1,128)S(1)}, f32[1,640]{1,0:T(1,128)S(1)}, u32[]{:S(2)}, u32[]{:S(2)}) collective-permute-start(f32[1,640]{1,0:T(1,128)S(1)} %get-tuple-element.88), channel_id=1, source_target_pairs={{8,0},{16,8},{24,16},{32,24},{40,32},{48,40},{56,48},{64,56},{72,6... | collective-permute-start | bytes 7688 | tf_op jit(solution)/shard_map/ppermute | solution.py:27
  267.4 5.9 %collective-permute-start.15 = (f32[16,1]{1,0:T(8,128)S(1)}, f32[16,1]{1,0:T(8,128)S(1)}, u32[]{:S(2)}, u32[]{:S(2)}) collective-permute-start(f32[16,1]{1,0:T(8,128)S(1)} %get-tuple-element.87), channel_id=1, source_target_pairs={{0,1},{1,2},{2,3},{3,4},{4,5},{5,6},{6,7},{7,0},{8,9},{9,10},{10,1... | collective-permute-start | bytes 200 | tf_op jit(solution)/shard_map/ppermute | solution.py:26
  271.2 5.0 %collective-permute-start.14 = (f32[16,1]{1,0:T(8,128)S(1)}, f32[16,1]{1,0:T(8,128)S(1)}, u32[]{:S(2)}, u32[]{:S(2)}) collective-permute-start(f32[16,1]{1,0:T(8,128)S(1)} %get-tuple-element.86), channel_id=1, source_target_pairs={{1,0},{2,1},{3,2},{4,3},{5,4},{6,5},{7,6},{0,7},{9,8},{10,9},{11,1... | collective-permute-start | bytes 200 | tf_op jit(solution)/shard_map/ppermute | solution.py:27
where the time goes:
time: 333 us; the launch traced here: 332 us
  blocking collectives  194 us (58%)
  starting transfers between devices  84.6 us (25%)
  waiting for transfers between devices  17.3 us (5%)
  matrix products  12.9 us (4%)
  between operations  9.63 us (3%)
  other arithmetic  9 us (3%)
  local copies, waits for them, and re-layouts  4.19 us (1%)
    psum x20, blocking collectives, one_axis_at_a_time(): return functools.reduce(lax.psum, axes, x)  194 us
    ppermute x8, starting transfers between devices, with_halo(): lax.ppermute(leading, axis, [(b, a) for a, b in up])  63.4 us
    ppermute x8, starting transfers between devices, with_halo(): lax.ppermute(last, axis, up)  21.3 us
    ppermute x8, waiting for transfers between devices, with_halo(): lax.ppermute(leading, axis, [(b, a) for a, b in up])  9.96 us
    ppermute x8, waiting for transfers between devices, with_halo(): lax.ppermute(last, axis, up)  7.29 us
  transfers between devices with their start and end apart: 16, of which 6 were waited for; matrix products, arithmetic and copies ran while one was open for 0% of the time, Pallas kernels for 0%

commit v1 on v0

v1 whole, which is shorter than its diff:
```python
import functools

import jax
import jax.numpy as jnp
from jax import lax
from jax.experimental import pallas as pl
from jax.experimental.pallas import tpu as pltpu
from jax.sharding import Mesh
from jax.sharding import PartitionSpec as P

LAT = ("lat_0", "lat_1", "lat_2")
LON = ("lon_0", "lon_1")
AXES = LAT + LON
MESH = pl.DeviceIdType.MESH
HIGHEST = lax.Precision.HIGHEST

K = 16
DEPTH = 4
NY = 16
NX = 640
WIDE = NX + 128
ROWS = NY + 2 * DEPTH
NAT = NY + 16
WET, EAST, NORTH, SURF, RHS, GUESS = range(6)

f32 = jnp.float32


def far_first(n):
    return sorted(range(1, n), key=lambda d: -min(d, n - d))


def iota(shape, axis):
    return lax.broadcasted_iota(jnp.int32, shape, axis)


def kernel(
    sizes,
    rhs_hbm,
    guess_hbm,
    mask_hbm,
    east_hbm,
    north_hbm,
    surf_hbm,
    rec_hbm,
    x_out,
    r_out,
    vec,
    img1,
    img2,
    img3,
    nat,
    cen,
    ke,
    kw,
    kn,
    ks,
    st,
    res,
    mask_v,
    pack_vec,
    got_vec,
    pack_nat,
    got_nat,
    grams,
    ar_send,
    ar_a,
    ar_b,
    ar_c,
    comb,
    in_sem,
    halo_send,
    halo_recv,
    ssem_a,
    ssem_b,
    ssem_c,
    rsem_a,
    rsem_b,
    rsem_c,
):
    ny_dev, nzh, nx_dev, nzl, ncore = sizes
    my_y = lax.axis_index("lat_0")
    my_zh = lax.axis_index("lat_1")
    my_x = lax.axis_index("lat_2")
    my_zl = lax.axis_index("lon_0")
    my_c = lax.axis_index("lon_1")
    n_lat = ny_dev * nzh * nx_dev
    n_lon = nzl * ncore
    my_lat = (my_y * nzh + my_zh) * nx_dev + my_x
    my_lon = my_zl * ncore + my_c
    na, nb, nc = nx_dev * ncore, ny_dev, nzh * nzl
    my_a = my_x * ncore + my_c
    my_z = my_zh * nzl + my_zl

    def at_lat(index):
        index = lax.rem(index + n_lat, n_lat)
        rest = index // nx_dev
        return (rest // nzh, lax.rem(rest, nzh), lax.rem(index, nx_dev), my_zl, my_c)

    def at_lon(index):
        index = lax.rem(index + n_lon, n_lon)
        return (my_y, my_zh, my_x, index // ncore, lax.rem(index, ncore))

    def at_a(index):
        return (my_y, my_zh, index // ncore, my_zl, lax.rem(index, ncore))

    def at_b(index):
        return (index, my_zh, my_x, my_zl, my_c)

    def at_c(index):
        return (my_y, index // nzl, my_x, lax.rem(index, nzl), my_c)

    plain = (
        (east_hbm, EAST),
        (north_hbm, NORTH),
        (surf_hbm, SURF),
        (rhs_hbm, RHS),
        (guess_hbm, GUESS),
    )
    loads = [pltpu.make_async_copy(mask_hbm, mask_v, in_sem.at[0])]
    for i, (src, field) in enumerate(plain):
        loads.append(
            pltpu.make_async_copy(
                src, nat.at[field, pl.ds(8, NY), pl.ds(0, NX)], in_sem.at[1 + i]
            )
        )
    for k in range(K):
        loads.append(
            pltpu.make_async_copy(
                rec_hbm.at[k], vec.at[pl.ds(DEPTH, NY), k, pl.ds(0, NX)], in_sem.at[6 + k]
            )
        )
    for load in loads:
        load.start()

    nat[:, 0:8, :] = jnp.zeros((6, 8, WIDE), f32)
    nat[:, 24:32, :] = jnp.zeros((6, 8, WIDE), f32)
    nat[:, 8:24, NX:] = jnp.zeros((6, NY, 128), f32)
    res[...] = jnp.zeros(res.shape, f32)

    barrier = pltpu.get_barrier_semaphore()
    peers = [at_lat(my_lat + 1), at_lat(my_lat - 1), at_lon(my_lon + 1), at_lon(my_lon - 1)]
    for n, me, at in ((nc, my_z, at_c), (nb, my_y, at_b), (na, my_a, at_a)):
        for d in far_first(n):
            peers.append(at(lax.rem(me + d, n)))
    for peer in peers:
        pl.semaphore_signal(barrier, inc=1, device_id=peer, device_id_type=MESH)
    for load in loads:
        load.wait()
    nat[WET, 8:24, 0:NX] = mask_v[...].astype(f32)
    pl.semaphore_wait(barrier, len(peers))

    def remote(src, dst, at, slot):
        return pltpu.make_async_remote_copy(
            src_ref=src,
            dst_ref=dst,
            send_sem=halo_send.at[slot],
            recv_sem=halo_recv.at[slot],
            device_id=at,
            device_id_type=MESH,
        )

    north_of, south_of = at_lat(my_lat + 1), at_lat(my_lat - 1)
    east_of, west_of = at_lon(my_lon + 1), at_lon(my_lon - 1)
    lanes = pl.ds(0, NX)
    lat_copies = [
        remote(
            vec.at[pl.ds(NY, DEPTH), :, lanes], vec.at[pl.ds(0, DEPTH), :, lanes], north_of, 0
        ),
        remote(
            vec.at[pl.ds(DEPTH, DEPTH), :, lanes],
            vec.at[pl.ds(NY + DEPTH, DEPTH), :, lanes],
            south_of,
            1,
        ),
        remote(
            nat.at[:, pl.ds(20, DEPTH), lanes], nat.at[:, pl.ds(4, DEPTH), lanes], north_of, 2
        ),
        remote(
            nat.at[:, pl.ds(8, DEPTH), lanes], nat.at[:, pl.ds(24, DEPTH), lanes], south_of, 3
        ),
    ]
    for copy in lat_copies:
        copy.start()
    for copy in lat_copies:
        copy.wait()

    lane16 = iota((K, 128), 1)

    def pack_row(e, carry):
        to_west, to_east = carry
        mine = (lane16 >= DEPTH * e) & (lane16 < DEPTH * e + DEPTH)
        first = pltpu.roll(vec[e, :, 0:128], DEPTH * e, 1)
        last = pltpu.roll(vec[e, :, NX - 128 : NX], lax.rem(DEPTH * e + DEPTH, 128), 1)
        return jnp.where(mine, first, to_west), jnp.where(mine, last, to_east)

    zero16 = jnp.zeros((K, 128), f32)
    to_west, to_east = lax.fori_loop(0, ROWS, pack_row, (zero16, zero16))
    pack_vec[0] = to_west
    pack_vec[1] = to_east
    lane_n = iota((NAT, 128), 1)
    west_n = jnp.zeros((NAT, 128), f32)
    east_n = jnp.zeros((NAT, 128), f32)
    for i in range(6):
        mine = (lane_n >= DEPTH * i) & (lane_n < DEPTH * i + DEPTH)
        first = nat[i, :, 0:128]
        if i:
            first = pltpu.roll(first, DEPTH * i, 1)
        last = pltpu.roll(nat[i, :, NX - 128 : NX], DEPTH * i + DEPTH, 1)
        west_n = jnp.where(mine, first, west_n)
        east_n = jnp.where(mine, last, east_n)
    pack_nat[0] = west_n
    pack_nat[1] = east_n
    lon_copies = [
        remote(pack_vec.at[0], got_vec.at[0], west_of, 4),
        remote(pack_vec.at[1], got_vec.at[1], east_of, 5),
        remote(pack_nat.at[0], got_nat.at[0], west_of, 6),
        remote(pack_nat.at[1], got_nat.at[1], east_of, 7),
    ]
    for copy in lon_copies:
        copy.start()
    for copy in lon_copies:
        copy.wait()

    def unpack_row(e, carry):
        from_east = pltpu.roll(got_vec[0], lax.rem(128 - DEPTH * e, 128), 1)
        from_west = pltpu.roll(got_vec[1], 128 - DEPTH - DEPTH * e, 1)
        vec[e, :, NX:] = jnp.where(
            lane16 < DEPTH, from_east, jnp.where(lane16 >= 128 - DEPTH, from_west, 0.0)
        )
        return carry

    lax.fori_loop(0, ROWS, unpack_row, 0)
    for i in range(6):
        from_east = got_nat[0]
        if i:
            from_east = pltpu.roll(from_east, 128 - DEPTH * i, 1)
        from_west = pltpu.roll(got_nat[1], 128 - DEPTH - DEPTH * i, 1)
        nat[i, :, NX:] = jnp.where(
            lane_n < DEPTH, from_east, jnp.where(lane_n >= 128 - DEPTH, from_west, 0.0)
        )

    row_n = iota((NAT, WIDE), 0)
    beyond = ((row_n < 8) & (my_lat == 0)) | ((row_n >= 24) & (my_lat == n_lat - 1))

    def east(v):
        return pltpu.roll(v, WIDE - 1, 1)

    def west(v):
        return pltpu.roll(v, 1, 1)

    def north(v):
        return pltpu.roll(v, NAT - 1, 0)

    def south(v):
        return pltpu.roll(v, 1, 0)

    wet = jnp.where(beyond, 0.0, nat[WET])
    k_east = nat[EAST] * wet * east(wet)
    k_north = nat[NORTH] * wet * north(wet)
    k_west = west(k_east)
    k_south = south(k_north)
    ke[...] = k_east
    kw[...] = k_west
    kn[...] = k_north
    ks[...] = k_south
    cen[...] = nat[SURF] * wet + k_east + k_west + k_north + k_south + (1.0 - wet)

    def operate(v):
        return cen[...] * v - (
            ke[...] * east(v) + kw[...] * west(v) + kn[...] * north(v) + ks[...] * south(v)
        )

    def operate_vectors(src, dst, first, last):
        def row(e, carry):
            at = pl.ds(e + 4, 1)
            v = src[e]
            dst[e] = cen[at, :] * v - (
                ke[at, :] * east(v)
                + kw[at, :] * west(v)
                + kn[at, :] * src[e + 1]
                + ks[at, :] * src[e - 1]
            )
            return carry

        lax.fori_loop(first, last + 1, row, 0)

    st[...] = nat[RHS] - operate(nat[GUESS])
    operate_vectors(vec, img1, 1, 22)
    operate_vectors(img1, img2, 3, 20)
    operate_vectors(img2, img3, 4, 19)

    def fold(v):
        total = v[:, 0:128]
        for i in range(1, NX // 128):
            total = total + v[:, 128 * i : 128 * i + 128]
        return total

    def gram_row(y, carry):
        acc, start = carry
        e = y + DEPTH
        w, b1, b2, b3 = (ref[e, :, 0:NX] for ref in (vec, img1, img2, img3))
        left = jnp.concatenate([w, b1, b2], axis=0)
        right = jnp.concatenate([w, b1, b2, b3], axis=0)
        acc = acc + lax.dot_general(
            left, right, (((1,), (1,)), ((), ())), precision=HIGHEST, preferred_element_type=f32
        )
        return acc, start + fold(w * st[pl.ds(y + 8, 1), 0:NX])

    acc, start = lax.fori_loop(0, NY, gram_row, (jnp.zeros((3 * K, 4 * K), f32), zero16))
    grams[...] = jnp.zeros(grams.shape, f32)
    grams[:, 0 : 4 * K] = acc

    def block(i, j, lane):
        v = grams[K * i : K * i + K, :]
        v = jnp.where((lane16 >= K * j) & (lane16 < K * j + K), v, 0.0)
        shift = (lane - K * j) % 128
        return pltpu.roll(v, shift, 1) if shift else v

    payload = 0.5 * (block(0, 1, 0) + block(1, 0, 0))
    payload = payload + block(1, 1, 16) + block(1, 2, 32) + block(2, 2, 48) + block(2, 3, 64)
    payload = jnp.where(lane16 == 80, jnp.sum(start, axis=1, keepdims=True), payload)

    def phase(turn, step, value, buf, ssem, rsem, n, me, at):
        ar_send[turn, step] = value
        buf[turn, me] = value
        for d in far_first(n):
            pltpu.make_async_remote_copy(
                src_ref=ar_send.at[turn, step],
                dst_ref=buf.at[turn, me],
                send_sem=ssem.at[turn, d],
                recv_sem=rsem.at[turn, me],
                device_id=at(lax.rem(me + d, n)),
                device_id_type=MESH,
            ).start()
        for d in range(1, n):
            peer = lax.rem(me + d, n)
            pltpu.make_async_remote_copy(
                src_ref=ar_send.at[turn, step],
                dst_ref=buf.at[turn, peer],
                send_sem=ssem.at[turn, d],
                recv_sem=rsem.at[turn, peer],
                device_id=at(peer),
                device_id_type=MESH,
            ).wait()
        total = buf[turn, 0]
        for i in range(1, n):
            total = total + buf[turn, i]
        return total

    def all_reduce(turn, value):
        value = phase(turn, 0, value, ar_a, ssem_a, rsem_a, na, my_a, at_a)
        value = phase(turn, 1, value, ar_b, ssem_b, rsem_b, nb, my_y, at_b)
        return phase(turn, 2, value, ar_c, ssem_c, rsem_c, nc, my_z, at_c)

    sums = all_reduce(0, payload)

    sub16 = iota((K, 128), 0)
    aug = jnp.where(lane16 < K, sums, 0.0)
    aug = jnp.where(lane16 == sub16 + K, 1.0, aug)
    aug = jnp.where(lane16 == 2 * K, sums[:, 80:81], aug)
    for i in range(K):
        pivot_row = aug[i : i + 1, :] / aug[i : i + 1, i : i + 1]
        aug = jnp.where(sub16 == i, pivot_row, aug - aug[:, i : i + 1] * pivot_row)
    coarse = aug[:, 2 * K : 2 * K + 1]

    def at_zero(v, lane):
        v = jnp.where((lane16 >= lane) & (lane16 < lane + K), v, 0.0)
        return pltpu.roll(v, (128 - lane) % 128, 1) if lane else v

    inverse = at_zero(aug, K)
    g2, g3, g4, g5 = (at_zero(sums, lane) for lane in (16, 32, 48, 64))

    def residual_row(e, carry):
        along = jnp.sum(coarse * img1[e], axis=0, keepdims=True)
        res[0, pl.ds(e + 4, 1), :] = st[pl.ds(e + 4, 1), :] - along
        return carry

    lax.fori_loop(1, 23, residual_row, 0)
    for i in range(3):
        res[i + 1] = operate(res[i])

    def moment_row(y, carry):
        e = y + DEPTH
        b1, b2 = img1[e, :, 0:NX], img2[e, :, 0:NX]
        r0, r1, r2, r3 = (res[i, pl.ds(y + 8, 1), 0:NX] for i in range(4))
        terms = (b1 * r0, b1 * r1, b1 * r2, b2 * r2, b2 * r3)
        return tuple(total + fold(term) for total, term in zip(carry, terms))

    defl = lax.fori_loop(0, NY, moment_row, (zero16,) * 5)
    payload = zero16
    for i, total in enumerate(defl):
        payload = jnp.where(lane16 == i, jnp.sum(total, axis=1, keepdims=True), payload)
    inner = [res[i, 8:24, 0:NX] for i in range(4)]
    for i, (a, b) in enumerate(((0, 0), (0, 1), (1, 1), (1, 2), (2, 2), (2, 3))):
        dot = jnp.sum(fold(inner[a] * inner[b]), axis=1, keepdims=True)
        payload = jnp.where(lane16 == 5 + i, dot, payload)

    sums = all_reduce(1, payload)
    d = [sums[:, i : i + 1] for i in range(5)]
    t = [jnp.sum(sums[:, 5 + i : 6 + i], axis=0, keepdims=True) for i in range(6)]

    def apply(mat, col):
        row = jnp.sum(jnp.where(lane16 == sub16, col, 0.0), axis=0, keepdims=True)
        return jnp.sum(mat * row, axis=1, keepdims=True)

    def dot(a, b):
        return jnp.sum(a * b, axis=0, keepdims=True)

    mu0 = apply(inverse, d[0])
    g2_0, g3_0, g4_0, g5_0 = (apply(g, mu0) for g in (g2, g3, g4, g5))
    defl1 = d[1] - g2_0
    mu1 = apply(inverse, defl1)
    g2_1, g3_1 = apply(g2, mu1), apply(g3, mu1)
    defl2 = d[2] - g3_0 - g2_1
    mu2 = apply(inverse, defl2)
    m = [
        t[0],
        t[1] - dot(mu0, d[0]),
        t[2] - 2.0 * dot(mu0, d[1]) + dot(mu0, g2_0),
        t[3] - 2.0 * dot(mu0, d[2]) + dot(mu0, g3_0) - dot(mu1, defl1),
        t[4]
        - 2.0 * (dot(mu0, d[3]) + dot(mu1, d[2]))
        + dot(mu0, g4_0)
        + 2.0 * dot(mu1, g3_0)
        + dot(mu1, g2_1),
        t[5]
        - 2.0 * (dot(mu0, d[4]) + dot(mu1, d[3]))
        + dot(mu0, g5_0)
        + 2.0 * dot(mu1, g4_0)
        + dot(mu1, g3_1)
        - dot(mu2, defl2),
    ]

    def form(poly, shift):
        total = 0.0
        for i, a in enumerate(poly):
            for j, b in enumerate(poly):
                total = total + a * b * m[i + j + shift]
        return total

    one = jnp.ones((1, 1), f32)
    zero = jnp.zeros((1, 1), f32)
    r_poly = [one]
    y_poly = [zero]
    zeta = [zero, zero, zero]
    curv = prev_norm = one
    for turn in range(3):
        norm = form(r_poly, 0)
        r_image = form(r_poly, 1)
        if turn == 0:
            y_poly = list(r_poly)
            curv = r_image
        else:
            ratio = norm / prev_norm
            y_poly = [a + ratio * b for a, b in zip(r_poly, y_poly + [zero])]
            curv = r_image - ratio * ratio * curv
        step_len = norm / curv
        for i, a in enumerate(y_poly):
            zeta[i] = zeta[i] + step_len * a
        r_poly = [
            a - step_len * b for a, b in zip(r_poly + [zero], [zero] + list(y_poly))
        ]
        prev_norm = norm

    nu2 = zeta[2] * mu0
    nu1 = zeta[1] * mu0 + zeta[2] * mu1
    nu0 = zeta[0] * mu0 + zeta[1] * mu1 + zeta[2] * mu2
    x_w = coarse - nu0

    def final_row(y, carry):
        e = y + DEPTH
        w, b1, b2, b3 = (ref[e, :, 0:NX] for ref in (vec, img1, img2, img3))
        at = pl.ds(y, 1)
        comb[0, at, :] = jnp.sum(x_w * w - nu1 * b1 - nu2 * b2, axis=0, keepdims=True)
        comb[1, at, :] = jnp.sum(nu0 * b1 + nu1 * b2 + nu2 * b3, axis=0, keepdims=True)
        return carry

    lax.fori_loop(0, NY, final_row, 0)
    x_out[...] = (
        nat[GUESS, 8:24, 0:NX]
        + comb[0]
        + (zeta[0] * inner[0] + zeta[1] * inner[1] + zeta[2] * inner[2])
    )
    r_out[...] = inner[0] - (
        zeta[0] * inner[1] + zeta[1] * inner[2] + zeta[2] * inner[3] - comb[1]
    )


def shards(right_side, first_guess, cell_mask, cond_east, cond_north, surface, recycled):
    sizes = tuple(lax.axis_size(axis) for axis in AXES)
    ny_dev, nzh, nx_dev, nzl, ncore = sizes
    na, nb, nc = nx_dev * ncore, ny_dev, nzh * nzl
    field = jax.ShapeDtypeStruct((NY, NX), f32)
    vmem = pltpu.VMEM
    dma = pltpu.SemaphoreType.DMA
    plain = vmem((NAT, WIDE), f32)
    return pl.pallas_call(
        functools.partial(kernel, sizes),
        out_shape=(field, field),
        in_specs=[pl.BlockSpec(memory_space=pl.ANY)] * 7,
        out_specs=(pl.BlockSpec(memory_space=pltpu.VMEM),) * 2,
        scratch_shapes=[vmem((ROWS, K, WIDE), f32)] * 4
        + [vmem((6, NAT, WIDE), f32)]
        + [plain] * 6
        + [
            vmem((4, NAT, WIDE), f32),
            vmem((NY, NX), jnp.int32),
            vmem((2, K, 128), f32),
            vmem((2, K, 128), f32),
            vmem((2, NAT, 128), f32),
            vmem((2, NAT, 128), f32),
            vmem((3 * K, 128), f32),
            vmem((2, 3, K, 128), f32),
            vmem((2, na, K, 128), f32),
            vmem((2, nb, K, 128), f32),
            vmem((2, nc, K, 128), f32),
            vmem((2, NY, NX), f32),
            dma((22,)),
            dma((8,)),
            dma((8,)),
            dma((2, na)),
            dma((2, nb)),
            dma((2, nc)),
            dma((2, na)),
            dma((2, nb)),
            dma((2, nc)),
        ],
        compiler_params=pltpu.CompilerParams(collective_id=0, has_side_effects=True),
    )(right_side, first_guess, cell_mask, cond_east, cond_north, surface, recycled)


def finer_mesh(mesh):
    return Mesh(mesh.devices.reshape(8, 3, 4, 4, 2), AXES)


def solution(mesh):
    in_specs = (P(LAT, LON),) * 6 + (P(None, LAT, LON),)
    out_specs = (P(LAT, LON), P(LAT, LON))
    return jax.shard_map(
        shards, mesh=finer_mesh(mesh), in_specs=in_specs, out_specs=out_specs, check_vma=False
    )
```

time: 333 us -> 101 us (0.30)
  blocking collectives: 194 us -> 0 us
  Pallas kernels: 0 us -> 97.6 us
  starting transfers between devices: 84.6 us -> 0 us
  waiting for transfers between devices: 17.3 us -> 0 us
  matrix products: 12.9 us -> 0 us
  other arithmetic: 9 us -> 0 us
  between operations: 9.63 us -> 0.65 us
    psum x20 -> x0, blocking collectives: 194 us -> none  [one_axis_at_a_time(): return functools.reduce(lax.psum, axes, x)]
    pallas_call x0 -> x1, Pallas kernels: none -> 97.6 us  [shards(): pl.pallas_call(functools.partial(kernel, sizes), out_shape=(field, field)...]
    ppermute x16 -> x0, starting transfers between devices: 84.6 us -> none  [the longest x8 63.4 us: with_halo(): lax.ppermute(leading, axis, [(b, a) for a, b in up])]
    ppermute x16 -> x0, waiting for transfers between devices: 17.3 us -> none  [the longest x8 9.96 us: with_halo(): lax.ppermute(leading, axis, [(b, a) for a, b in up])]
    dot_general x13 -> x0, matrix products: 9.97 us -> none  [the longest x3 2.84 us: shards(): defl_local = jnp.einsum('kyx,yx->k', recycled, image_res, precision=PRECISE)]
    another operation x5 -> x0, other arithmetic: 4.01 us -> none  [the longest x3 2.13 us: shards(): factor = jnp.linalg.cholesky(0.5 * (gram + gram.T))]
  transfers between devices with their start and end apart: 16 -> 0, of which waited for: 6 -> 0; matrix products, arithmetic and copies ran while one was open for 0% -> 0% of each run, Pallas kernels for 0% -> 0%
where the time goes in v1:
time: 101 us; the launch traced here: 100 us
  Pallas kernels  97.6 us (97%)
  local copies, waits for them, and re-layouts  2.03 us (2%)
    pallas_call x1, Pallas kernels, shards(): pl.pallas_call(functools.partial(kernel, sizes), out_shape=(field, field)...  97.6 us
    unnamed x4, local copies, waits for them, and re-layouts  2.03 us

profile of v1, /device:TPU:1, one launch (start us, length us, event | category | flops | bytes accessed | tf_op | source)
XLA Modules:
  0.0 100.3 jit_solution(1745316760725939279)
XLA Ops:
  0.6 97.6 %shard_map.86 = (f32[16,640]{1,0:T(8,128)}, f32[16,640]{1,0:T(8,128)}) custom-call(f32[16,640]{1,0:T(8,128)} %rhs_hbm.1, f32[16,640]{1,0:T(8,128)} %guess_hbm.1, s32[16,640]{1,0:T(8,128)} %mask_hbm.1, f32[16,640]{1,0:T(8,128)} %east_hbm.1, f32[16,640]{1,0:T(8,128)} %north_hbm.1, f32[16,640]{1,0:T(8,128)} %surf_hbm.1, f32[16,16,640]{2,1,0:T(8,128)} %rec_hbm.1), custom_call_target="tpu_custom_call" | custom-call | tf_op jit(solution)/shard_map/pallas_call | solution.py:498
  98.2 0.0 copy-start
  98.2 1.4 %copy.11 = f32[16,640]{1,0:T(8,128)} copy(f32[16,640]{1,0:T(8,128)} %get-tuple-element.4) | data formatting | bytes 81920
  99.6 0.0 copy-done
  99.6 0.6 copy.12
Async XLA Ops:
  98.2 1.4 %copy-start = (f32[16,640]{1,0:T(8,128)S(1)}, f32[16,640]{1,0:T(8,128)}, u32[]{:S(2)}) copy-start(f32[16,640]{1,0:T(8,128)} %get-tuple-element.5) | copy-start | bytes 122884

commit v2 on v1

v2 whole, which is shorter than its diff:
```python
import functools

import jax
import jax.numpy as jnp
from jax import lax
from jax.experimental import pallas as pl
from jax.experimental.pallas import tpu as pltpu
from jax.sharding import Mesh
from jax.sharding import PartitionSpec as P

LAT = ("lat_0", "lat_1", "lat_2")
LON = ("lon_0", "lon_1")
AXES = LAT + LON
MESH = pl.DeviceIdType.MESH
HIGHEST = lax.Precision.HIGHEST

K = 16
DEPTH = 3
NY = 16
NX = 640
WIDE = NX + 128
ROWS = NY + 2
NAT = NY + 16
WET, NORTH, GUESS, EAST, SURF, RHS = range(6)

f32 = jnp.float32


def far_first(n):
    return sorted(range(1, n), key=lambda d: -min(d, n - d))


def iota(shape, axis):
    return lax.broadcasted_iota(jnp.int32, shape, axis)


def kernel(
    sizes,
    rhs_hbm,
    guess_hbm,
    mask_hbm,
    east_hbm,
    north_hbm,
    surf_hbm,
    rec_hbm,
    x_out,
    r_out,
    vec,
    img1,
    img2,
    nat,
    land,
    coef,
    st,
    res,
    mask_v,
    pack_vec,
    got_vec,
    pack_nat,
    got_nat,
    got_tile,
    got_corner,
    ar_send,
    ar_a,
    ar_b,
    ar_c,
    ar_d,
    ar_e,
    comb,
    in_sem,
    halo_send,
    halo_recv,
    ssem_a,
    ssem_b,
    ssem_c,
    ssem_d,
    ssem_e,
    rsem_a,
    rsem_b,
    rsem_c,
    rsem_d,
    rsem_e,
):
    ny_dev, nzh, nx_dev, nzl, ncore = sizes
    my_y = lax.axis_index("lat_0")
    my_zh = lax.axis_index("lat_1")
    my_x = lax.axis_index("lat_2")
    my_zl = lax.axis_index("lon_0")
    my_c = lax.axis_index("lon_1")
    n_lat = ny_dev * nzh * nx_dev
    n_lon = nzl * ncore
    my_lat = (my_y * nzh + my_zh) * nx_dev + my_x
    my_lon = my_zl * ncore + my_c
    na, nb, nc = nx_dev * ncore, ny_dev, nzh * nzl
    nd, ne = nx_dev * ny_dev, nzh * nzl * ncore
    my_a = my_x * ncore + my_c
    my_z = my_zh * nzl + my_zl
    my_d = my_y * nx_dev + my_x
    my_e = my_z * ncore + my_c

    def at_cell(up, right):
        lat = lax.rem(my_lat + (up + n_lat), n_lat)
        lon = lax.rem(my_lon + (right + n_lon), n_lon)
        rest = lat // nx_dev
        return (
            rest // nzh,
            lax.rem(rest, nzh),
            lax.rem(lat, nx_dev),
            lon // ncore,
            lax.rem(lon, ncore),
        )

    def at_a(index):
        return (my_y, my_zh, index // ncore, my_zl, lax.rem(index, ncore))

    def at_b(index):
        return (index, my_zh, my_x, my_zl, my_c)

    def at_c(index):
        return (my_y, index // nzl, my_x, lax.rem(index, nzl), my_c)

    def at_d(index):
        return (index // nx_dev, my_zh, lax.rem(index, nx_dev), my_zl, my_c)

    def at_e(index):
        z = index // ncore
        return (my_y, z // nzl, my_x, lax.rem(z, nzl), lax.rem(index, ncore))

    north_of, south_of = at_cell(1, 0), at_cell(-1, 0)
    east_of, west_of = at_cell(0, 1), at_cell(0, -1)
    corners = (at_cell(1, 1), at_cell(1, -1), at_cell(-1, 1), at_cell(-1, -1))

    plain = (
        (east_hbm, EAST),
        (north_hbm, NORTH),
        (surf_hbm, SURF),
        (rhs_hbm, RHS),
        (guess_hbm, GUESS),
    )
    loads = [pltpu.make_async_copy(mask_hbm, mask_v, in_sem.at[0])]
    for i, (src, field) in enumerate(plain):
        loads.append(
            pltpu.make_async_copy(
                src, nat.at[field, pl.ds(8, NY), pl.ds(0, NX)], in_sem.at[1 + i]
            )
        )
    for k in range(K):
        loads.append(
            pltpu.make_async_copy(
                rec_hbm.at[k], vec.at[pl.ds(1, NY), k, pl.ds(0, NX)], in_sem.at[6 + k]
            )
        )
    for load in loads:
        load.start()

    nat[:, 0:8, :] = jnp.zeros((6, 8, WIDE), f32)
    nat[:, 24:32, :] = jnp.zeros((6, 8, WIDE), f32)
    nat[:, 8:24, NX:] = jnp.zeros((6, NY, 128), f32)
    res[:, 0:8, :] = jnp.zeros((4, 8, WIDE), f32)
    res[:, 24:32, :] = jnp.zeros((4, 8, WIDE), f32)

    barrier = pltpu.get_barrier_semaphore()
    peers = [north_of, south_of, *corners, east_of, west_of]
    for n, me, at in ((ne, my_e, at_e), (nd, my_d, at_d), (na, my_a, at_a)):
        for d in far_first(n):
            peers.append(at(lax.rem(me + d, n)))
    for peer in peers:
        pl.semaphore_signal(barrier, inc=1, device_id=peer, device_id_type=MESH)
    for load in loads:
        load.wait()
    nat[WET, 8:24, 0:NX] = mask_v[...].astype(f32)

    def remote(src, dst, at, slot):
        return pltpu.make_async_remote_copy(
            src_ref=src,
            dst_ref=dst,
            send_sem=halo_send.at[slot],
            recv_sem=halo_recv.at[slot],
            device_id=at,
            device_id_type=MESH,
        )

    def start_all(copies):
        for copy in copies:
            copy.start()

    def wait_all(copies):
        for copy in copies:
            copy.wait()

    lanes = pl.ds(0, NX)
    lane16 = iota((K, 128), 1)
    sub16 = iota((K, 128), 0)
    lane_n = iota((NAT, 128), 1)
    zero16 = jnp.zeros((K, 128), f32)

    def pack_vectors(ref, turn):
        def row(y, carry):
            to_west, to_east = carry
            first = pltpu.roll(ref[y + 1, :, 0:128], y, 1)
            last = pltpu.roll(ref[y + 1, :, NX - 128 : NX], y + 1, 1)
            mine = lane16 == y
            return jnp.where(mine, first, to_west), jnp.where(mine, last, to_east)

        to_west, to_east = lax.fori_loop(0, NY, row, (zero16, zero16), unroll=4)
        pack_vec[turn, 0] = to_west
        pack_vec[turn, 1] = to_east

    def unpack_vectors(ref, turn):
        def row(y, carry):
            from_east = pltpu.roll(got_vec[turn, 0], lax.rem(128 - y, 128), 1)
            from_west = pltpu.roll(got_vec[turn, 1], 127 - y, 1)
            ref[y + 1, :, NX:] = jnp.where(
                lane16 == 0, from_east, jnp.where(lane16 == 127, from_west, 0.0)
            )
            return carry

        lax.fori_loop(0, NY, row, 0, unroll=4)

    def vector_rows(ref, slot):
        return [
            remote(ref.at[NY, :, lanes], ref.at[0, :, lanes], north_of, slot),
            remote(ref.at[1, :, lanes], ref.at[NY + 1, :, lanes], south_of, slot + 1),
        ]

    def vector_columns(turn, slot):
        return [
            remote(pack_vec.at[turn, 0], got_vec.at[turn, 0], west_of, slot),
            remote(pack_vec.at[turn, 1], got_vec.at[turn, 1], east_of, slot + 1),
        ]

    def landed(first, count, near, far):
        for i in range(first, first + count):
            nat[i, 8 - far : 9 - near, 0:NX] = land[i, 8 - far : 9 - near, :]
            nat[i, 23 + near : 24 + far, 0:NX] = land[i, 23 + near : 24 + far, :]

    def pack_plain(turn):
        to_west = jnp.zeros((NAT, 128), f32)
        to_east = jnp.zeros((NAT, 128), f32)
        for i in range(5):
            mine = (lane_n >= DEPTH * i) & (lane_n < DEPTH * i + DEPTH)
            first = nat[i, :, 0:128]
            if i:
                first = pltpu.roll(first, DEPTH * i, 1)
            last = pltpu.roll(nat[i, :, NX - 128 : NX], DEPTH * i + DEPTH, 1)
            to_west = jnp.where(mine, first, to_west)
            to_east = jnp.where(mine, last, to_east)
        pack_nat[turn, 0] = to_west
        pack_nat[turn, 1] = to_east

    def unpack_plain(turn):
        for i in range(5):
            from_east = got_nat[turn, 0]
            if i:
                from_east = pltpu.roll(from_east, 128 - DEPTH * i, 1)
            from_west = pltpu.roll(got_nat[turn, 1], 128 - DEPTH - DEPTH * i, 1)
            nat[i, :, NX:] = jnp.where(
                lane_n < DEPTH, from_east, jnp.where(lane_n >= 128 - DEPTH, from_west, 0.0)
            )

    def plain_columns(turn, slot):
        return [
            remote(pack_nat.at[turn, 0], got_nat.at[turn, 0], west_of, slot),
            remote(pack_nat.at[turn, 1], got_nat.at[turn, 1], east_of, slot + 1),
        ]

    def plain_rows(first, count, near, far, slot):
        fields, n = pl.ds(first, count), far - near + 1
        return [
            remote(
                nat.at[fields, pl.ds(24 - far, n), lanes],
                land.at[fields, pl.ds(8 - far, n)],
                north_of,
                slot,
            ),
            remote(
                nat.at[fields, pl.ds(7 + near, n), lanes],
                land.at[fields, pl.ds(23 + near, n)],
                south_of,
                slot + 1,
            ),
        ]

    pack_vectors(vec, 0)
    pack_plain(0)
    pl.semaphore_wait(barrier, len(peers))

    near_rows = plain_rows(0, 3, 1, 1, 0)
    vec_rows = vector_rows(vec, 2)
    vec_columns = vector_columns(0, 4)
    near_columns = plain_columns(0, 6)
    start_all(near_rows)
    start_all(vec_rows)
    start_all(near_columns)
    start_all(vec_columns)

    def east(v):
        return pltpu.roll(v, WIDE - 1, 1)

    def west(v):
        return pltpu.roll(v, 1, 1)

    def north(v):
        return pltpu.roll(v, NAT - 1, 0)

    def south(v):
        return pltpu.roll(v, 1, 0)

    def coefficients():
        row_n = iota((NAT, WIDE), 0)
        beyond = ((row_n < 8) & (my_lat == 0)) | ((row_n >= 24) & (my_lat == n_lat - 1))
        wet = jnp.where(beyond, 0.0, nat[WET])
        k_east = nat[EAST] * wet * east(wet)
        k_north = nat[NORTH] * wet * north(wet)
        k_west = west(k_east)
        k_south = south(k_north)
        coef[1] = k_east
        coef[2] = k_west
        coef[3] = k_north
        coef[4] = k_south
        coef[0] = nat[SURF] * wet + k_east + k_west + k_north + k_south + (1.0 - wet)

    def operate(v):
        return coef[0] * v - (
            coef[1] * east(v) + coef[2] * west(v) + coef[3] * north(v) + coef[4] * south(v)
        )

    def image_row(src, dst, y):
        at = pl.ds(y + 8, 1)
        v = src[y + 1]
        out = coef[0, at, :] * v - (
            coef[1, at, :] * east(v)
            + coef[2, at, :] * west(v)
            + coef[3, at, :] * src[y + 2]
            + coef[4, at, :] * src[y]
        )
        dst[y + 1, :, 0:NX] = out[:, 0:NX]
        return out[:, 0:NX]

    def fold(v):
        total = v[:, 0:128]
        for i in range(1, NX // 128):
            total = total + v[:, 128 * i : 128 * i + 128]
        return total

    def contract(a, b):
        return lax.dot_general(
            a, b, (((1,), (1,)), ((), ())), precision=HIGHEST, preferred_element_type=f32
        )

    def first_pair(rows, carry):
        acc, w_s, b_s = carry
        both = []
        for y in rows:
            w = vec[y + 1, :, 0:NX]
            b = image_row(vec, img1, y)
            s = st[pl.ds(y + 8, 1), 0:NX]
            w_s = w_s + fold(w * s)
            b_s = b_s + fold(b * s)
            both.append(jnp.concatenate([w, b], axis=0))
        both = jnp.concatenate(both, axis=1)
        return acc + contract(both, both), w_s, b_s

    def start_residual():
        st[...] = nat[RHS] - operate(nat[GUESS])

    wait_all(near_columns)
    unpack_plain(0)
    coefficients()
    start_residual()
    wait_all(vec_columns)
    unpack_vectors(vec, 0)
    carry = (jnp.zeros((2 * K, 2 * K), f32), zero16, zero16)
    carry = lax.fori_loop(
        0, NY // 2 - 1, lambda i, c: first_pair((2 * i + 1, 2 * i + 2), c), carry
    )
    wait_all(near_rows)
    landed(0, 3, 1, 1)
    wait_all(vec_rows)
    coefficients()
    start_residual()
    acc, w_s, b_s = first_pair((0, NY - 1), carry)

    def put(block, lane):
        wide = jnp.concatenate([block, jnp.zeros((K, 128 - block.shape[1]), f32)], axis=1)
        return pltpu.roll(wide, lane, 1) if lane else wide

    def column(payload, lane, total):
        return jnp.where(lane16 == lane, jnp.sum(total, axis=1, keepdims=True), payload)

    def pack(v, width):
        per, shift = 128 // width, width
        while shift < 128:
            v = v + pltpu.roll(v, shift, 1)
            shift *= 2
        v = jnp.where(lane16 // width == lax.rem(sub16, per), v, 0.0)
        return [
            jnp.sum(jnp.where(sub16 // per == i, v, 0.0), axis=0, keepdims=True)
            for i in range(K // per)
        ]

    def unpack(rows, width):
        per, shift = 128 // width, width
        v = jnp.broadcast_to(rows[0], (K, 128))
        for i in range(1, K // per):
            v = jnp.where(sub16 // per == i, rows[i], v)
        v = jnp.where(lane16 // width == lax.rem(sub16, per), v, 0.0)
        while shift < 128:
            v = v + pltpu.roll(v, shift, 1)
            shift *= 2
        return jnp.where(lane16 < width, v, 0.0)

    def send_phase(phase, value):
        send, buf, ssem, rsem, n, me, at, count = phase
        if count == 1:
            send[0:1, :] = value
            src, dst = send.at[pl.ds(0, 1)], buf.at[pl.ds(me, 1)]
        else:
            for i, row in enumerate(value):
                send[i : i + 1, :] = row
            src, dst = send.at[pl.ds(0, count)], buf.at[me, pl.ds(0, count)]
        for d in far_first(n):
            pltpu.make_async_remote_copy(
                src_ref=src,
                dst_ref=dst,
                send_sem=ssem.at[d],
                recv_sem=rsem.at[me],
                device_id=at(lax.rem(me + d, n)),
                device_id_type=MESH,
            ).start()
        if count == 1:
            buf[pl.ds(me, 1), :] = value
        else:
            for i, row in enumerate(value):
                buf[me, i : i + 1, :] = row

    def wait_phase(phase):
        send, buf, ssem, rsem, n, me, at, count = phase
        for d in range(1, n):
            peer = lax.rem(me + d, n)
            if count == 1:
                src, dst = send.at[pl.ds(0, 1)], buf.at[pl.ds(peer, 1)]
            else:
                src, dst = send.at[pl.ds(0, count)], buf.at[peer, pl.ds(0, count)]
            pltpu.make_async_remote_copy(
                src_ref=src,
                dst_ref=dst,
                send_sem=ssem.at[d],
                recv_sem=rsem.at[peer],
                device_id=at(peer),
                device_id_type=MESH,
            ).wait()
        if count == 1:
            return jnp.sum(buf[...], axis=0, keepdims=True)
        total = buf[0]
        for i in range(1, n):
            total = total + buf[i]
        return [total[i : i + 1, :] for i in range(count)]

    def three_phases(turn, count):
        return (
            (ar_send.at[turn, 0], ar_a.at[turn], ssem_a.at[turn], rsem_a.at[turn], na, my_a, at_a, count),
            (ar_send.at[turn, 1], ar_b.at[turn], ssem_b.at[turn], rsem_b.at[turn], nb, my_y, at_b, count),
            (ar_send.at[turn, 2], ar_c.at[turn], ssem_c.at[turn], rsem_c.at[turn], nc, my_z, at_c, count),
        )

    two_phases = (
        (ar_send.at[2, 0], ar_d, ssem_d, rsem_d, nd, my_d, at_d, 1),
        (ar_send.at[2, 1], ar_e, ssem_e, rsem_e, ne, my_e, at_e, 1),
    )

    def all_reduce(phases, value, between):
        for step, phase in enumerate(phases):
            send_phase(phase, value)
            if between[step] is not None:
                between[step]()
            value = wait_phase(phase)
        return value

    g3_phases = three_phases(1, 2)
    deep_rows = plain_rows(0, 2, 2, DEPTH, 8) + plain_rows(3, 2, 1, DEPTH, 10)
    deep_columns = plain_columns(1, 12)
    img_rows = vector_rows(img1, 14)
    img_columns = vector_columns(1, 16)

    def between_a():
        start_all(deep_rows)
        start_all(img_rows)
        pack_vectors(img1, 1)
        start_all(img_columns)

    def between_b():
        wait_all(deep_rows)
        landed(0, 2, 2, DEPTH)
        landed(3, 2, 1, DEPTH)
        pack_plain(1)
        start_all(deep_columns)
        wait_all(img_columns)
        unpack_vectors(img1, 1)

    kept = {}

    def second_pair(rows, acc):
        left, right = [], []
        for y in rows:
            left.append(img1[y + 1, :, 0:NX])
            right.append(image_row(img1, img2, y))
        left, right = jnp.concatenate(left, axis=1), jnp.concatenate(right, axis=1)
        return acc + contract(left, right)

    def between_c():
        acc = jnp.zeros((K, K), f32)
        acc = lax.fori_loop(
            0, NY // 2 - 1, lambda i, c: second_pair((2 * i + 1, 2 * i + 2), c), acc
        )
        wait_all(img_rows)
        kept["g3"] = second_pair((0, NY - 1), acc)
        send_phase(g3_phases[0], pack(put(kept["g3"], 0), K))
        wait_all(deep_columns)
        unpack_plain(1)
        coefficients()

    grams = 0.5 * (put(acc[0:K, K:], 0) + put(acc[K:, 0:K], 0)) + put(acc[K:, K:], K)
    rows = pack(grams, 2 * K) + pack(column(column(zero16, 0, w_s), 1, b_s), 8)
    rows = all_reduce(three_phases(0, 5), rows, (between_a, between_b, between_c))
    grams = unpack(rows[0:4], 2 * K)
    starts = unpack(rows[4:5], 8)


    def at_zero(v, lane):
        v = jnp.where((lane16 >= lane) & (lane16 < lane + K), v, 0.0)
        return pltpu.roll(v, (128 - lane) % 128, 1) if lane else v

    aug = jnp.where(lane16 < K, grams, 0.0)
    aug = jnp.where(lane16 == sub16 + K, 1.0, aug)
    aug = jnp.where(lane16 == 2 * K, starts[:, 0:1], aug)
    for i in range(K):
        pivot_row = aug[i : i + 1, :] / aug[i : i + 1, i : i + 1]
        aug = jnp.where(sub16 == i, pivot_row, aug - aug[:, i : i + 1] * pivot_row)
    coarse = aug[:, 2 * K : 2 * K + 1]
    inverse = at_zero(aug, K)
    g2 = at_zero(grams, K)

    def apply(mat, col):
        row = jnp.sum(jnp.where(lane16 == sub16, col, 0.0), axis=0, keepdims=True)
        return jnp.sum(mat * row, axis=1, keepdims=True)

    def dot(a, b):
        return jnp.sum(a * b, axis=0, keepdims=True)

    mu0 = apply(inverse, starts[:, 1:2] - apply(g2, coarse))


    def residual_row(y):
        at = pl.ds(y + 8, 1)
        r = st[at, 0:NX] - jnp.sum(coarse * img1[y + 1, :, 0:NX], axis=0, keepdims=True)
        comb[0, pl.ds(y, 1), :] = r
        res[0, at, 0:NX] = r - jnp.sum(mu0 * vec[y + 1, :, 0:NX], axis=0, keepdims=True)

    for y in range(DEPTH):
        residual_row(y)
        residual_row(NY - DEPTH + y)
    first = res.at[0]
    dir_rows = [
        remote(first.at[pl.ds(20, 4), lanes], first.at[pl.ds(4, 4), lanes], north_of, 18),
        remote(first.at[pl.ds(8, 4), lanes], first.at[pl.ds(24, 4), lanes], south_of, 19),
    ]
    left, right = pl.ds(0, 128), pl.ds(NX - 128, 128)
    dir_corners = [
        remote(first.at[pl.ds(16, 8), right], got_corner.at[0], corners[0], 20),
        remote(first.at[pl.ds(16, 8), left], got_corner.at[1], corners[1], 21),
        remote(first.at[pl.ds(8, 8), right], got_corner.at[2], corners[2], 22),
        remote(first.at[pl.ds(8, 8), left], got_corner.at[3], corners[3], 23),
    ]
    dir_columns = [
        remote(first.at[pl.ds(8, NY), left], got_tile.at[0], west_of, 24),
        remote(first.at[pl.ds(8, NY), right], got_tile.at[1], east_of, 25),
    ]
    residual_row(DEPTH)
    residual_row(NY - DEPTH - 1)
    start_all(dir_rows)

    def inner_row(y, carry):
        residual_row(y)
        return carry

    lax.fori_loop(DEPTH + 1, NY - DEPTH - 1, inner_row, 0, unroll=4)
    start_all(dir_corners)
    start_all(dir_columns)
    g3_rows = wait_phase(g3_phases[0])
    send_phase(g3_phases[1], g3_rows)
    wait_all(dir_columns)
    wait_all(dir_corners)
    wait_all(dir_rows)
    lane8 = lane16[0:8]

    def edge_columns(from_east, from_west, lane):
        return jnp.where(
            lane < DEPTH, from_east, jnp.where(lane >= 128 - DEPTH, from_west, 0.0)
        )

    res[0, 8:24, NX:] = edge_columns(got_tile[0], got_tile[1], lane16)
    res[0, 0:8, NX:] = edge_columns(got_corner[1], got_corner[0], lane8)
    res[0, 24:32, NX:] = edge_columns(got_corner[3], got_corner[2], lane8)
    for i in range(3):
        res[i + 1] = operate(res[i])

    def moment_row(y, carry):
        e = y + 1
        b1, b2 = img1[e, :, 0:NX], img2[e, :, 0:NX]
        v1, a1 = (res[i, pl.ds(y + 8, 1), 0:NX] for i in (1, 2))
        terms = (b1 * v1, b1 * a1, b2 * a1)
        return tuple(total + fold(term) for total, term in zip(carry, terms))

    defl = lax.fori_loop(0, NY, moment_row, (zero16,) * 3, unroll=2)
    payload = zero16
    for i, total in enumerate(defl):
        payload = column(payload, i, total)
    inner = [comb[0]] + [res[i, 8:24, 0:NX] for i in (1, 2, 3)]
    for i, (a, b) in enumerate(((0, 0), (0, 1), (1, 1), (1, 2), (2, 2), (2, 3))):
        total = jnp.sum(fold(inner[a] * inner[b]), axis=0, keepdims=True)
        total = jnp.sum(total, axis=1, keepdims=True)
        payload = jnp.where((lane16 == 3) & (sub16 == i), total, payload)

    def before_scalars():
        def row(y, carry):
            at = pl.ds(y + 8, 1)
            along = jnp.sum(coarse * vec[y + 1, :, 0:NX], axis=0, keepdims=True)
            st[at, 0:NX] = nat[GUESS, at, 0:NX] + along
            return carry

        lax.fori_loop(0, NY, row, 0, unroll=4)
        send_phase(g3_phases[2], wait_phase(g3_phases[1]))

    def last_gram():
        kept["g3"] = unpack(wait_phase(g3_phases[2]), K)

    row = all_reduce(two_phases, pack(payload, 8)[0], (before_scalars, last_gram))
    sums = unpack([row], 8)

    g3 = kept["g3"]
    e = [sums[:, i : i + 1] for i in range(3)]
    t = [sums[i : i + 1, 3:4] for i in range(6)]
    mu1 = apply(inverse, e[0])
    g2_1, g3_1 = apply(g2, mu1), apply(g3, mu1)
    defl2 = e[1] - g2_1
    mu2 = apply(inverse, defl2)
    m = [
        t[0],
        t[1],
        t[2],
        t[3] - dot(mu1, e[0]),
        t[4] - 2.0 * dot(mu1, e[1]) + dot(mu1, g2_1),
        t[5] - 2.0 * dot(mu1, e[2]) + dot(mu1, g3_1) - dot(mu2, defl2),
    ]

    def form(poly, shift):
        total = 0.0
        for i, a in enumerate(poly):
            for j, b in enumerate(poly):
                total = total + a * b * m[i + j + shift]
        return total

    one = jnp.ones((1, 1), f32)
    zero = jnp.zeros((1, 1), f32)
    r_poly = [one]
    y_poly = [zero]
    zeta = [zero, zero, zero]
    curv = prev_norm = one
    for turn in range(3):
        norm = form(r_poly, 0)
        r_image = form(r_poly, 1)
        if turn == 0:
            y_poly = list(r_poly)
            curv = r_image
        else:
            ratio = norm / prev_norm
            y_poly = [a + ratio * b for a, b in zip(r_poly, y_poly + [zero])]
            curv = r_image - ratio * ratio * curv
        step_len = norm / curv
        for i, a in enumerate(y_poly):
            zeta[i] = zeta[i] + step_len * a
        r_poly = [
            a - step_len * b for a, b in zip(r_poly + [zero], [zero] + list(y_poly))
        ]
        prev_norm = norm

    along_w = zeta[1] * mu1 + zeta[2] * mu2
    along_b = zeta[2] * mu1

    def final_row(y, carry):
        w, b1, b2 = (ref[y + 1, :, 0:NX] for ref in (vec, img1, img2))
        at = pl.ds(y, 1)
        comb[1, at, :] = jnp.sum(along_w * w + along_b * b1, axis=0, keepdims=True)
        comb[2, at, :] = jnp.sum(along_w * b1 + along_b * b2, axis=0, keepdims=True)
        return carry

    lax.fori_loop(0, NY, final_row, 0, unroll=4)
    p0, v1, a1, a2 = (res[i, 8:24, 0:NX] for i in range(4))
    x_out[...] = (
        st[8:24, 0:NX] + (zeta[0] * p0 + zeta[1] * v1 + zeta[2] * a1) - comb[1]
    )
    r_out[...] = comb[0] - (zeta[0] * v1 + zeta[1] * a1 + zeta[2] * a2) + comb[2]


def shards(right_side, first_guess, cell_mask, cond_east, cond_north, surface, recycled):
    sizes = tuple(lax.axis_size(axis) for axis in AXES)
    ny_dev, nzh, nx_dev, nzl, ncore = sizes
    na, nb, nc = nx_dev * ncore, ny_dev, nzh * nzl
    nd, ne = nx_dev * ny_dev, nzh * nzl * ncore
    field = jax.ShapeDtypeStruct((NY, NX), f32)
    vmem = pltpu.VMEM
    dma = pltpu.SemaphoreType.DMA
    return pl.pallas_call(
        functools.partial(kernel, sizes),
        out_shape=(field, field),
        in_specs=[pl.BlockSpec(memory_space=pl.ANY)] * 7,
        out_specs=(pl.BlockSpec(memory_space=pltpu.VMEM),) * 2,
        scratch_shapes=[
            vmem((ROWS, K, WIDE), f32),
            vmem((ROWS, K, WIDE), f32),
            vmem((ROWS, K, NX), f32),
            vmem((6, NAT, WIDE), f32),
            vmem((5, NAT, NX), f32),
            vmem((5, NAT, WIDE), f32),
            vmem((NAT, WIDE), f32),
            vmem((4, NAT, WIDE), f32),
            vmem((NY, NX), jnp.int32),
            vmem((2, 2, K, 128), f32),
            vmem((2, 2, K, 128), f32),
            vmem((2, 2, NAT, 128), f32),
            vmem((2, 2, NAT, 128), f32),
            vmem((2, NY, 128), f32),
            vmem((4, 8, 128), f32),
            vmem((3, 3, 8, 128), f32),
            vmem((2, na, 8, 128), f32),
            vmem((2, nb, 8, 128), f32),
            vmem((2, nc, 8, 128), f32),
            vmem((nd, 128), f32),
            vmem((ne, 128), f32),
            vmem((3, NY, NX), f32),
            dma((22,)),
            dma((26,)),
            dma((26,)),
            dma((2, na)),
            dma((2, nb)),
            dma((2, nc)),
            dma((nd,)),
            dma((ne,)),
            dma((2, na)),
            dma((2, nb)),
            dma((2, nc)),
            dma((nd,)),
            dma((ne,)),
        ],
        compiler_params=pltpu.CompilerParams(collective_id=0, has_side_effects=True),
    )(right_side, first_guess, cell_mask, cond_east, cond_north, surface, recycled)


def finer_mesh(mesh):
    return Mesh(mesh.devices.reshape(8, 3, 4, 4, 2), AXES)


def solution(mesh):
    in_specs = (P(LAT, LON),) * 6 + (P(None, LAT, LON),)
    out_specs = (P(LAT, LON), P(LAT, LON))
    return jax.shard_map(
        shards, mesh=finer_mesh(mesh), in_specs=in_specs, out_specs=out_specs, check_vma=False
    )
```

time: 101 us -> 73.9 us (0.73)
  Pallas kernels: 97.6 us -> 71 us
    pallas_call x1, Pallas kernels: 97.6 us -> 71 us  [shards(): pl.pallas_call(functools.partial(kernel, sizes), out_shape=(field, field)...]
where the time goes in v2:
time: 73.9 us; the launch traced here: 73.6 us
  Pallas kernels  71 us (96%)
  local copies, waits for them, and re-layouts  2.03 us (3%)
    pallas_call x1, Pallas kernels, shards(): pl.pallas_call(functools.partial(kernel, sizes), out_shape=(field, field)...  71 us
    unnamed x4, local copies, waits for them, and re-layouts  2.03 us

profile of v2, /device:TPU:1, one launch (start us, length us, event | category | flops | bytes accessed | tf_op | source)
XLA Modules:
  0.0 73.6 jit_solution(14006416555254519953)
XLA Ops:
  0.6 71.0 %shard_map.86 = (f32[16,640]{1,0:T(8,128)}, f32[16,640]{1,0:T(8,128)}) custom-call(f32[16,640]{1,0:T(8,128)} %rhs_hbm.1, f32[16,640]{1,0:T(8,128)} %guess_hbm.1, s32[16,640]{1,0:T(8,128)} %mask_hbm.1, f32[16,640]{1,0:T(8,128)} %east_hbm.1, f32[16,640]{1,0:T(8,128)} %north_hbm.1, f32[16,640]{1,0:T(8,128)} %surf_hbm.1, f32[16,16,640]{2,1,0:T(8,128)} %rec_hbm.1), custom_call_target="tpu_custom_call" | custom-call | tf_op jit(solution)/shard_map/pallas_call | solution.py:714
  71.6 0.0 copy-start
  71.6 1.4 %copy.11 = f32[16,640]{1,0:T(8,128)} copy(f32[16,640]{1,0:T(8,128)} %get-tuple-element.4) | data formatting | bytes 81920
  73.0 0.0 copy-done
  73.0 0.6 copy.12
Async XLA Ops:
  71.6 1.4 %copy-start = (f32[16,640]{1,0:T(8,128)S(1)}, f32[16,640]{1,0:T(8,128)}, u32[]{:S(2)}) copy-start(f32[16,640]{1,0:T(8,128)} %get-tuple-element.5) | copy-start | bytes 122884

commit v3 on v2

--- a/solution.py
+++ b/solution.py
@@ -15,11 +15,11 @@
 HIGHEST = lax.Precision.HIGHEST
 
 K = 16
-DEPTH = 3
+DEPTH = 4
 NY = 16
 NX = 640
 WIDE = NX + 128
-ROWS = NY + 2
+ROWS = NY + 2 * DEPTH
 NAT = NY + 16
 WET, NORTH, GUESS, EAST, SURF, RHS = range(6)
 
@@ -58,8 +58,6 @@
     got_vec,
     pack_nat,
     got_nat,
-    got_tile,
-    got_corner,
     ar_send,
     ar_a,
     ar_b,
@@ -67,6 +65,7 @@
     ar_d,
     ar_e,
     comb,
+    relay,
     in_sem,
     halo_send,
     halo_recv,
@@ -130,6 +129,14 @@
     east_of, west_of = at_cell(0, 1), at_cell(0, -1)
     corners = (at_cell(1, 1), at_cell(1, -1), at_cell(-1, 1), at_cell(-1, -1))
 
+    barrier = pltpu.get_barrier_semaphore()
+    peers = [north_of, south_of, *corners, east_of, west_of]
+    for n, me, at in ((ne, my_e, at_e), (nd, my_d, at_d), (na, my_a, at_a)):
+        for d in far_first(n):
+            peers.append(at(lax.rem(me + d, n)))
+    for peer in peers:
+        pl.semaphore_signal(barrier, inc=1, device_id=peer, device_id_type=MESH)
+
     plain = (
         (east_hbm, EAST),
         (north_hbm, NORTH),
@@ -147,7 +154,7 @@
     for k in range(K):
         loads.append(
             pltpu.make_async_copy(
-                rec_hbm.at[k], vec.at[pl.ds(1, NY), k, pl.ds(0, NX)], in_sem.at[6 + k]
+                rec_hbm.at[k], vec.at[pl.ds(DEPTH, NY), k, pl.ds(0, NX)], in_sem.at[6 + k]
             )
         )
     for load in loads:
@@ -156,16 +163,9 @@
     nat[:, 0:8, :] = jnp.zeros((6, 8, WIDE), f32)
     nat[:, 24:32, :] = jnp.zeros((6, 8, WIDE), f32)
     nat[:, 8:24, NX:] = jnp.zeros((6, NY, 128), f32)
-    res[:, 0:8, :] = jnp.zeros((4, 8, WIDE), f32)
-    res[:, 24:32, :] = jnp.zeros((4, 8, WIDE), f32)
-
-    barrier = pltpu.get_barrier_semaphore()
-    peers = [north_of, south_of, *corners, east_of, west_of]
-    for n, me, at in ((ne, my_e, at_e), (nd, my_d, at_d), (na, my_a, at_a)):
-        for d in far_first(n):
-            peers.append(at(lax.rem(me + d, n)))
-    for peer in peers:
-        pl.semaphore_signal(barrier, inc=1, device_id=peer, device_id_type=MESH)
+    res[:, 0:8, :] = jnp.zeros((5, 8, WIDE), f32)
+    res[:, 24:32, :] = jnp.zeros((5, 8, WIDE), f32)
+
     for load in loads:
         load.wait()
     nat[WET, 8:24, 0:NX] = mask_v[...].astype(f32)
@@ -191,77 +191,165 @@
     lanes = pl.ds(0, NX)
     lane16 = iota((K, 128), 1)
     sub16 = iota((K, 128), 0)
-    lane_n = iota((NAT, 128), 1)
     zero16 = jnp.zeros((K, 128), f32)
 
-    def pack_vectors(ref, turn):
+    def pack_vectors():
         def row(y, carry):
             to_west, to_east = carry
-            first = pltpu.roll(ref[y + 1, :, 0:128], y, 1)
-            last = pltpu.roll(ref[y + 1, :, NX - 128 : NX], y + 1, 1)
-            mine = lane16 == y
+            e, lane = y + DEPTH, DEPTH * y
+            first = pltpu.roll(vec[e, :, 0:128], lane, 1)
+            last = pltpu.roll(vec[e, :, NX - 128 : NX], lane + DEPTH, 1)
+            mine = (lane16 >= lane) & (lane16 < lane + DEPTH)
             return jnp.where(mine, first, to_west), jnp.where(mine, last, to_east)
 
         to_west, to_east = lax.fori_loop(0, NY, row, (zero16, zero16), unroll=4)
-        pack_vec[turn, 0] = to_west
-        pack_vec[turn, 1] = to_east
-
-    def unpack_vectors(ref, turn):
-        def row(y, carry):
-            from_east = pltpu.roll(got_vec[turn, 0], lax.rem(128 - y, 128), 1)
-            from_west = pltpu.roll(got_vec[turn, 1], 127 - y, 1)
-            ref[y + 1, :, NX:] = jnp.where(
-                lane16 == 0, from_east, jnp.where(lane16 == 127, from_west, 0.0)
-            )
+        pack_vec[0] = to_west
+        pack_vec[1] = to_east
+
+    def edge_columns(from_east, from_west, lane):
+        return jnp.where(
+            lane < DEPTH, from_east, jnp.where(lane >= 128 - DEPTH, from_west, 0.0)
+        )
+
+    def unpack_vectors(first, count, y0, place):
+        def row(i, carry):
+            lane = DEPTH * (y0 + i)
+            from_east = pltpu.roll(got_vec[place], lax.rem(128 - lane, 128), 1)
+            from_west = pltpu.roll(got_vec[place + 1], 128 - DEPTH - lane, 1)
+            vec[first + i, :, NX:] = edge_columns(from_east, from_west, lane16)
             return carry
 
-        lax.fori_loop(0, NY, row, 0, unroll=4)
-
-    def vector_rows(ref, slot):
-        return [
-            remote(ref.at[NY, :, lanes], ref.at[0, :, lanes], north_of, slot),
-            remote(ref.at[1, :, lanes], ref.at[NY + 1, :, lanes], south_of, slot + 1),
-        ]
-
-    def vector_columns(turn, slot):
-        return [
-            remote(pack_vec.at[turn, 0], got_vec.at[turn, 0], west_of, slot),
-            remote(pack_vec.at[turn, 1], got_vec.at[turn, 1], east_of, slot + 1),
-        ]
+        lax.fori_loop(0, count, row, 0, unroll=4)
+
+    def pack_plain():
+        to_west, to_east = zero16, zero16
+        for i in range(6):
+            lane = DEPTH * i
+            first, last = nat[i, 8:24, 0:128], nat[i, 8:24, NX - 128 : NX]
+            if i:
+                first = pltpu.roll(first, lane, 1)
+            last = pltpu.roll(last, lane + DEPTH, 1)
+            mine = (lane16 >= lane) & (lane16 < lane + DEPTH)
+            to_west = jnp.where(mine, first, to_west)
+            to_east = jnp.where(mine, last, to_east)
+        pack_nat[0] = to_west
+        pack_nat[1] = to_east
+
+    def unpack_plain(first, count, y0, place):
+        lane = lane16[0:count]
+        for i in range(6):
+            from_east = got_nat[place, y0 : y0 + count, :]
+            from_west = got_nat[place + 1, y0 : y0 + count, :]
+            if i:
+                from_east = pltpu.roll(from_east, 128 - DEPTH * i, 1)
+            from_west = pltpu.roll(from_west, 128 - DEPTH - DEPTH * i, 1)
+            nat[i, first : first + count, NX:] = edge_columns(from_east, from_west, lane)
 
     def landed(first, count, near, far):
         for i in range(first, first + count):
             nat[i, 8 - far : 9 - near, 0:NX] = land[i, 8 - far : 9 - near, :]
             nat[i, 23 + near : 24 + far, 0:NX] = land[i, 23 + near : 24 + far, :]
 
-    def pack_plain(turn):
-        to_west = jnp.zeros((NAT, 128), f32)
-        to_east = jnp.zeros((NAT, 128), f32)
-        for i in range(5):
-            mine = (lane_n >= DEPTH * i) & (lane_n < DEPTH * i + DEPTH)
-            first = nat[i, :, 0:128]
-            if i:
-                first = pltpu.roll(first, DEPTH * i, 1)
-            last = pltpu.roll(nat[i, :, NX - 128 : NX], DEPTH * i + DEPTH, 1)
-            to_west = jnp.where(mine, first, to_west)
-            to_east = jnp.where(mine, last, to_east)
-        pack_nat[turn, 0] = to_west
-        pack_nat[turn, 1] = to_east
-
-    def unpack_plain(turn):
-        for i in range(5):
-            from_east = got_nat[turn, 0]
-            if i:
-                from_east = pltpu.roll(from_east, 128 - DEPTH * i, 1)
-            from_west = pltpu.roll(got_nat[turn, 1], 128 - DEPTH - DEPTH * i, 1)
-            nat[i, :, NX:] = jnp.where(
-                lane_n < DEPTH, from_east, jnp.where(lane_n >= 128 - DEPTH, from_west, 0.0)
+    def vector_rows(near, far, slot):
+        n = far - near + 1
+        return [
+            remote(
+                vec.at[pl.ds(20 - far, n), :, lanes],
+                vec.at[pl.ds(4 - far, n), :, lanes],
+                north_of,
+                slot,
+            ),
+            remote(
+                vec.at[pl.ds(3 + near, n), :, lanes],
+                vec.at[pl.ds(19 + near, n), :, lanes],
+                south_of,
+                slot + 1,
+            ),
+        ]
+
+    def far_rows():
+        ahead, behind = lax.rem(my_zh + 1, nzh), lax.rem(my_zh + (nzh - 1), nzh)
+        next_y = jnp.where(my_zh == nzh - 1, lax.rem(my_y + 1, ny_dev), my_y)
+        last_y = jnp.where(my_zh == 0, lax.rem(my_y + (ny_dev - 1), ny_dev), my_y)
+        ways = (
+            (
+                my_x == nx_dev - 1,
+                my_x == 0,
+                vec.at[pl.ds(16, 2), :, lanes],
+                vec.at[pl.ds(0, 2), :, lanes],
+                north_of,
+                (next_y, my_zh, 0, my_zl, my_c),
+                (my_y, ahead, my_x, my_zl, my_c),
+            ),
+            (
+                my_x == 0,
+                my_x == nx_dev - 1,
+                vec.at[pl.ds(6, 2), :, lanes],
+                vec.at[pl.ds(22, 2), :, lanes],
+                south_of,
+                (last_y, my_zh, nx_dev - 1, my_zl, my_c),
+                (my_y, behind, my_x, my_zl, my_c),
+            ),
+        )
+
+        def copy(src, dst, at, send_slot, recv_slot):
+            return pltpu.make_async_remote_copy(
+                src_ref=src,
+                dst_ref=dst,
+                send_sem=halo_send.at[send_slot],
+                recv_sem=halo_recv.at[recv_slot],
+                device_id=at,
+                device_id_type=MESH,
             )
 
-    def plain_columns(turn, slot):
+        hops = []
+        for i, (crosses, forwards, src, dst, straight, first_hop, last_hop) in enumerate(ways):
+            held = relay.at[i]
+            hops.append(
+                (
+                    crosses,
+                    forwards,
+                    copy(src, dst, straight, 22 + i, 22 + i),
+                    copy(src, held, first_hop, 24 + i, 24 + i),
+                    copy(held, dst, last_hop, 26 + i, 22 + i),
+                )
+            )
+
+        def begin():
+            for crosses, _, straight, first, _ in hops:
+                pl.when(jnp.logical_not(crosses))(straight.start)
+                pl.when(crosses)(first.start)
+
+        def forward():
+            for _, forwards, _, first, last in hops:
+
+                @pl.when(forwards)
+                def _():
+                    first.wait_recv()
+                    last.start()
+
+        def finish():
+            for crosses, forwards, straight, first, last in hops:
+                pl.when(jnp.logical_not(crosses))(straight.wait_send)
+                pl.when(crosses)(first.wait_send)
+                pl.when(forwards)(last.wait_send)
+                straight.wait_recv()
+
+        return begin, forward, finish
+
+    def columns(pack, got, slot):
         return [
-            remote(pack_nat.at[turn, 0], got_nat.at[turn, 0], west_of, slot),
-            remote(pack_nat.at[turn, 1], got_nat.at[turn, 1], east_of, slot + 1),
+            remote(pack.at[0], got.at[0], west_of, slot),
+            remote(pack.at[1], got.at[1], east_of, slot + 1),
+        ]
+
+    def corner_columns(pack, got, slot, south_rows, north_rows):
+        north_east, north_west, south_east, south_west = corners
+        return [
+            remote(pack.at[0, south_rows], got.at[2, south_rows], south_west, slot),
+            remote(pack.at[1, south_rows], got.at[3, south_rows], south_east, slot + 1),
+            remote(pack.at[0, north_rows], got.at[4, north_rows], north_west, slot + 2),
+            remote(pack.at[1, north_rows], got.at[5, north_rows], north_east, slot + 3),
         ]
 
     def plain_rows(first, count, near, far, slot):
@@ -281,18 +369,27 @@
             ),
         ]
 
-    pack_vectors(vec, 0)
-    pack_plain(0)
+    pack_vectors()
+    pack_plain()
     pl.semaphore_wait(barrier, len(peers))
 
     near_rows = plain_rows(0, 3, 1, 1, 0)
-    vec_rows = vector_rows(vec, 2)
-    vec_columns = vector_columns(0, 4)
-    near_columns = plain_columns(0, 6)
+    vec_rows = vector_rows(1, 1, 2)
+    vec_columns = columns(pack_vec, got_vec, 4)
+    near_columns = columns(pack_nat, got_nat, 6)
+    all_rows = pl.ds(0, NY)
+    far = far_rows()
+    deep = (
+        corner_columns(pack_nat, got_nat, 18, pl.ds(0, 8), pl.ds(8, 8))
+        + plain_rows(0, 3, 2, DEPTH, 8)
+        + plain_rows(3, 3, 1, DEPTH - 1, 10)
+        + corner_columns(pack_vec, got_vec, 14, all_rows, all_rows)
+        + vector_rows(2, 2, 12)
+    )
+    start_all(near_columns)
+    start_all(vec_columns)
     start_all(near_rows)
     start_all(vec_rows)
-    start_all(near_columns)
-    start_all(vec_columns)
 
     def east(v):
         return pltpu.roll(v, WIDE - 1, 1)
@@ -325,17 +422,15 @@
             coef[1] * east(v) + coef[2] * west(v) + coef[3] * north(v) + coef[4] * south(v)
         )
 
-    def image_row(src, dst, y):
-        at = pl.ds(y + 8, 1)
-        v = src[y + 1]
-        out = coef[0, at, :] * v - (
+    def image_row(src, e):
+        at = pl.ds(e + 4, 1)
+        v = src[e]
+        return coef[0, at, :] * v - (
             coef[1, at, :] * east(v)
             + coef[2, at, :] * west(v)
-            + coef[3, at, :] * src[y + 2]
-            + coef[4, at, :] * src[y]
-        )
-        dst[y + 1, :, 0:NX] = out[:, 0:NX]
-        return out[:, 0:NX]
+            + coef[3, at, :] * src[e + 1]
+            + coef[4, at, :] * src[e - 1]
+        )
 
     def fold(v):
         total = v[:, 0:128]
@@ -352,8 +447,10 @@
         acc, w_s, b_s = carry
         both = []
         for y in rows:
-            w = vec[y + 1, :, 0:NX]
-            b = image_row(vec, img1, y)
+            w = vec[y + DEPTH, :, 0:NX]
+            image = image_row(vec, y + DEPTH)
+            img1[y + DEPTH] = image
+            b = image[:, 0:NX]
             s = st[pl.ds(y + 8, 1), 0:NX]
             w_s = w_s + fold(w * s)
             b_s = b_s + fold(b * s)
@@ -365,15 +462,17 @@
         st[...] = nat[RHS] - operate(nat[GUESS])
 
     wait_all(near_columns)
-    unpack_plain(0)
+    unpack_plain(8, NY, 0, 0)
     coefficients()
     start_residual()
     wait_all(vec_columns)
-    unpack_vectors(vec, 0)
+    unpack_vectors(DEPTH, NY, 0, 0)
+    far[0]()
     carry = (jnp.zeros((2 * K, 2 * K), f32), zero16, zero16)
     carry = lax.fori_loop(
         0, NY // 2 - 1, lambda i, c: first_pair((2 * i + 1, 2 * i + 2), c), carry
     )
+    start_all(deep)
     wait_all(near_rows)
     landed(0, 3, 1, 1)
     wait_all(vec_rows)
@@ -478,51 +577,47 @@
         return value
 
     g3_phases = three_phases(1, 2)
-    deep_rows = plain_rows(0, 2, 2, DEPTH, 8) + plain_rows(3, 2, 1, DEPTH, 10)
-    deep_columns = plain_columns(1, 12)
-    img_rows = vector_rows(img1, 14)
-    img_columns = vector_columns(1, 16)
-
-    def between_a():
-        start_all(deep_rows)
-        start_all(img_rows)
-        pack_vectors(img1, 1)
-        start_all(img_columns)
-
-    def between_b():
-        wait_all(deep_rows)
-        landed(0, 2, 2, DEPTH)
-        landed(3, 2, 1, DEPTH)
-        pack_plain(1)
-        start_all(deep_columns)
-        wait_all(img_columns)
-        unpack_vectors(img1, 1)
-
     kept = {}
 
     def second_pair(rows, acc):
         left, right = [], []
         for y in rows:
-            left.append(img1[y + 1, :, 0:NX])
-            right.append(image_row(img1, img2, y))
+            left.append(img1[y + DEPTH, :, 0:NX])
+            right.append(image_row(img1, y + DEPTH)[:, 0:NX])
+            img2[y] = right[-1]
         left, right = jnp.concatenate(left, axis=1), jnp.concatenate(right, axis=1)
         return acc + contract(left, right)
 
+    def between_a():
+        acc = jnp.zeros((K, K), f32)
+        kept["g3"] = lax.fori_loop(
+            0, NY // 2 - 1, lambda i, c: second_pair((2 * i + 1, 2 * i + 2), c), acc
+        )
+
     def between_c():
-        acc = jnp.zeros((K, K), f32)
-        acc = lax.fori_loop(
-            0, NY // 2 - 1, lambda i, c: second_pair((2 * i + 1, 2 * i + 2), c), acc
-        )
-        wait_all(img_rows)
-        kept["g3"] = second_pair((0, NY - 1), acc)
-        send_phase(g3_phases[0], pack(put(kept["g3"], 0), K))
-        wait_all(deep_columns)
-        unpack_plain(1)
+        wait_all(deep)
+        far[2]()
+        landed(0, 3, 2, DEPTH)
+        landed(3, 3, 1, DEPTH - 1)
+        unpack_plain(24, 8, 0, 2)
+        unpack_plain(0, 8, 8, 4)
+        unpack_vectors(NY + DEPTH, DEPTH, 0, 2)
+        unpack_vectors(0, DEPTH, NY - DEPTH, 4)
         coefficients()
+        start_residual()
+
+        def outer_row(i, carry):
+            img1[i + 1] = image_row(vec, i + 1)
+            img1[i + 19] = image_row(vec, i + 19)
+            return carry
+
+        lax.fori_loop(0, DEPTH, outer_row, 0)
+        acc = second_pair((0, NY - 1), kept["g3"])
+        send_phase(g3_phases[0], pack(put(acc, 0), K))
 
     grams = 0.5 * (put(acc[0:K, K:], 0) + put(acc[K:, 0:K], 0)) + put(acc[K:, K:], K)
     rows = pack(grams, 2 * K) + pack(column(column(zero16, 0, w_s), 1, b_s), 8)
-    rows = all_reduce(three_phases(0, 5), rows, (between_a, between_b, between_c))
+    rows = all_reduce(three_phases(0, 5), rows, (between_a, far[1], between_c))
     grams = unpack(rows[0:4], 2 * K)
     starts = unpack(rows[4:5], 8)
 
@@ -539,7 +634,7 @@
         aug = jnp.where(sub16 == i, pivot_row, aug - aug[:, i : i + 1] * pivot_row)
     coarse = aug[:, 2 * K : 2 * K + 1]
     inverse = at_zero(aug, K)
-    g2 = at_zero(grams, K)
+    g1, g2 = at_zero(grams, 0), at_zero(grams, K)
 
     def apply(mat, col):
         row = jnp.sum(jnp.where(lane16 == sub16, col, 0.0), axis=0, keepdims=True)
@@ -548,66 +643,24 @@
     def dot(a, b):
         return jnp.sum(a * b, axis=0, keepdims=True)
 
+    coarse = coarse + apply(inverse, starts[:, 0:1] - apply(g1, coarse))
     mu0 = apply(inverse, starts[:, 1:2] - apply(g2, coarse))
 
 
-    def residual_row(y):
-        at = pl.ds(y + 8, 1)
-        r = st[at, 0:NX] - jnp.sum(coarse * img1[y + 1, :, 0:NX], axis=0, keepdims=True)
-        comb[0, pl.ds(y, 1), :] = r
-        res[0, at, 0:NX] = r - jnp.sum(mu0 * vec[y + 1, :, 0:NX], axis=0, keepdims=True)
-
-    for y in range(DEPTH):
-        residual_row(y)
-        residual_row(NY - DEPTH + y)
-    first = res.at[0]
-    dir_rows = [
-        remote(first.at[pl.ds(20, 4), lanes], first.at[pl.ds(4, 4), lanes], north_of, 18),
-        remote(first.at[pl.ds(8, 4), lanes], first.at[pl.ds(24, 4), lanes], south_of, 19),
-    ]
-    left, right = pl.ds(0, 128), pl.ds(NX - 128, 128)
-    dir_corners = [
-        remote(first.at[pl.ds(16, 8), right], got_corner.at[0], corners[0], 20),
-        remote(first.at[pl.ds(16, 8), left], got_corner.at[1], corners[1], 21),
-        remote(first.at[pl.ds(8, 8), right], got_corner.at[2], corners[2], 22),
-        remote(first.at[pl.ds(8, 8), left], got_corner.at[3], corners[3], 23),
-    ]
-    dir_columns = [
-        remote(first.at[pl.ds(8, NY), left], got_tile.at[0], west_of, 24),
-        remote(first.at[pl.ds(8, NY), right], got_tile.at[1], east_of, 25),
-    ]
-    residual_row(DEPTH)
-    residual_row(NY - DEPTH - 1)
-    start_all(dir_rows)
-
-    def inner_row(y, carry):
-        residual_row(y)
+    def residual_row(e, carry):
+        at = pl.ds(e + 4, 1)
+        r = st[at, :] - jnp.sum(coarse * img1[e], axis=0, keepdims=True)
+        res[4, at, :] = r
+        res[0, at, :] = r - jnp.sum(mu0 * vec[e], axis=0, keepdims=True)
         return carry
 
-    lax.fori_loop(DEPTH + 1, NY - DEPTH - 1, inner_row, 0, unroll=4)
-    start_all(dir_corners)
-    start_all(dir_columns)
-    g3_rows = wait_phase(g3_phases[0])
-    send_phase(g3_phases[1], g3_rows)
-    wait_all(dir_columns)
-    wait_all(dir_corners)
-    wait_all(dir_rows)
-    lane8 = lane16[0:8]
-
-    def edge_columns(from_east, from_west, lane):
-        return jnp.where(
-            lane < DEPTH, from_east, jnp.where(lane >= 128 - DEPTH, from_west, 0.0)
-        )
-
-    res[0, 8:24, NX:] = edge_columns(got_tile[0], got_tile[1], lane16)
-    res[0, 0:8, NX:] = edge_columns(got_corner[1], got_corner[0], lane8)
-    res[0, 24:32, NX:] = edge_columns(got_corner[3], got_corner[2], lane8)
+    lax.fori_loop(1, ROWS - 1, residual_row, 0, unroll=2)
+    send_phase(g3_phases[1], wait_phase(g3_phases[0]))
     for i in range(3):
         res[i + 1] = operate(res[i])
 
     def moment_row(y, carry):
-        e = y + 1
-        b1, b2 = img1[e, :, 0:NX], img2[e, :, 0:NX]
+        b1, b2 = img1[y + DEPTH, :, 0:NX], img2[y]
         v1, a1 = (res[i, pl.ds(y + 8, 1), 0:NX] for i in (1, 2))
         terms = (b1 * v1, b1 * a1, b2 * a1)
         return tuple(total + fold(term) for total, term in zip(carry, terms))
@@ -616,7 +669,7 @@
     payload = zero16
     for i, total in enumerate(defl):
         payload = column(payload, i, total)
-    inner = [comb[0]] + [res[i, 8:24, 0:NX] for i in (1, 2, 3)]
+    inner = [res[i, 8:24, 0:NX] for i in (4, 1, 2, 3)]
     for i, (a, b) in enumerate(((0, 0), (0, 1), (1, 1), (1, 2), (2, 2), (2, 3))):
         total = jnp.sum(fold(inner[a] * inner[b]), axis=0, keepdims=True)
         total = jnp.sum(total, axis=1, keepdims=True)
@@ -625,7 +678,7 @@
     def before_scalars():
         def row(y, carry):
             at = pl.ds(y + 8, 1)
-            along = jnp.sum(coarse * vec[y + 1, :, 0:NX], axis=0, keepdims=True)
+            along = jnp.sum(coarse * vec[y + DEPTH, :, 0:NX], axis=0, keepdims=True)
             st[at, 0:NX] = nat[GUESS, at, 0:NX] + along
             return carry
 
@@ -689,18 +742,18 @@
     along_b = zeta[2] * mu1
 
     def final_row(y, carry):
-        w, b1, b2 = (ref[y + 1, :, 0:NX] for ref in (vec, img1, img2))
+        w, b1, b2 = vec[y + DEPTH, :, 0:NX], img1[y + DEPTH, :, 0:NX], img2[y]
         at = pl.ds(y, 1)
-        comb[1, at, :] = jnp.sum(along_w * w + along_b * b1, axis=0, keepdims=True)
-        comb[2, at, :] = jnp.sum(along_w * b1 + along_b * b2, axis=0, keepdims=True)
+        comb[0, at, :] = jnp.sum(along_w * w + along_b * b1, axis=0, keepdims=True)
+        comb[1, at, :] = jnp.sum(along_w * b1 + along_b * b2, axis=0, keepdims=True)
         return carry
 
     lax.fori_loop(0, NY, final_row, 0, unroll=4)
-    p0, v1, a1, a2 = (res[i, 8:24, 0:NX] for i in range(4))
+    p0, v1, a1, a2, r0 = (res[i, 8:24, 0:NX] for i in range(5))
     x_out[...] = (
-        st[8:24, 0:NX] + (zeta[0] * p0 + zeta[1] * v1 + zeta[2] * a1) - comb[1]
+        st[8:24, 0:NX] + (zeta[0] * p0 + zeta[1] * v1 + zeta[2] * a1) - comb[0]
     )
-    r_out[...] = comb[0] - (zeta[0] * v1 + zeta[1] * a1 + zeta[2] * a2) + comb[2]
+    r_out[...] = r0 - (zeta[0] * v1 + zeta[1] * a1 + zeta[2] * a2) + comb[1]
 
 
 def shards(right_side, first_guess, cell_mask, cond_east, cond_north, surface, recycled):
@@ -719,29 +772,28 @@
         scratch_shapes=[
             vmem((ROWS, K, WIDE), f32),
             vmem((ROWS, K, WIDE), f32),
-            vmem((ROWS, K, NX), f32),
+            vmem((NY, K, NX), f32),
             vmem((6, NAT, WIDE), f32),
-            vmem((5, NAT, NX), f32),
+            vmem((6, NAT, NX), f32),
             vmem((5, NAT, WIDE), f32),
             vmem((NAT, WIDE), f32),
-            vmem((4, NAT, WIDE), f32),
+            vmem((5, NAT, WIDE), f32),
             vmem((NY, NX), jnp.int32),
-            vmem((2, 2, K, 128), f32),
-            vmem((2, 2, K, 128), f32),
-            vmem((2, 2, NAT, 128), f32),
-            vmem((2, 2, NAT, 128), f32),
+            vmem((2, K, 128), f32),
+            vmem((6, K, 128), f32),
             vmem((2, NY, 128), f32),
-            vmem((4, 8, 128), f32),
+            vmem((6, NY, 128), f32),
             vmem((3, 3, 8, 128), f32),
             vmem((2, na, 8, 128), f32),
             vmem((2, nb, 8, 128), f32),
             vmem((2, nc, 8, 128), f32),
             vmem((nd, 128), f32),
             vmem((ne, 128), f32),
-            vmem((3, NY, NX), f32),
+            vmem((2, NY, NX), f32),
+            vmem((2, 2, K, NX), f32),
             dma((22,)),
-            dma((26,)),
-            dma((26,)),
+            dma((28,)),
+            dma((28,)),
             dma((2, na)),
             dma((2, nb)),
             dma((2, nc)),

time: 73.9 us -> 69.5 us (0.940)
  Pallas kernels: 71 us -> 66.6 us
    pallas_call x1, Pallas kernels: 71 us -> 66.6 us  [shards(): pl.pallas_call(functools.partial(kernel, sizes), out_shape=(field, field)...]
where the time goes in v3:
time: 69.5 us; the launch traced here: 69.3 us
  Pallas kernels  66.6 us (96%)
  local copies, waits for them, and re-layouts  2.03 us (3%)
    pallas_call x1, Pallas kernels, shards(): pl.pallas_call(functools.partial(kernel, sizes), out_shape=(field, field)...  66.6 us
    unnamed x4, local copies, waits for them, and re-layouts  2.03 us

profile of v3, /device:TPU:1, one launch (start us, length us, event | category | flops | bytes accessed | tf_op | source)
XLA Modules:
  0.0 69.3 jit_solution(12632847345354550741)
XLA Ops:
  0.6 66.6 %shard_map.86 = (f32[16,640]{1,0:T(8,128)}, f32[16,640]{1,0:T(8,128)}) custom-call(f32[16,640]{1,0:T(8,128)} %rhs_hbm.1, f32[16,640]{1,0:T(8,128)} %guess_hbm.1, s32[16,640]{1,0:T(8,128)} %mask_hbm.1, f32[16,640]{1,0:T(8,128)} %east_hbm.1, f32[16,640]{1,0:T(8,128)} %north_hbm.1, f32[16,640]{1,0:T(8,128)} %surf_hbm.1, f32[16,16,640]{2,1,0:T(8,128)} %rec_hbm.1), custom_call_target="tpu_custom_call" | custom-call | tf_op jit(solution)/shard_map/pallas_call | solution.py:767
  67.2 0.0 copy-start
  67.2 1.4 %copy.11 = f32[16,640]{1,0:T(8,128)} copy(f32[16,640]{1,0:T(8,128)} %get-tuple-element.4) | data formatting | bytes 81920
  68.6 0.0 copy-done
  68.6 0.6 copy.12
Async XLA Ops:
  67.2 1.4 %copy-start = (f32[16,640]{1,0:T(8,128)S(1)}, f32[16,640]{1,0:T(8,128)}, u32[]{:S(2)}) copy-start(f32[16,640]{1,0:T(8,128)} %get-tuple-element.5) | copy-start | bytes 122884

commit v4 on v3

--- a/solution.py
+++ b/solution.py
@@ -16,6 +16,7 @@
 
 K = 16
 DEPTH = 4
+SHIFT = 4.0
 NY = 16
 NX = 640
 WIDE = NX + 128
@@ -43,8 +44,7 @@
     north_hbm,
     surf_hbm,
     rec_hbm,
-    x_out,
-    r_out,
+    out,
     vec,
     img1,
     img2,
@@ -473,6 +473,7 @@
         0, NY // 2 - 1, lambda i, c: first_pair((2 * i + 1, 2 * i + 2), c), carry
     )
     start_all(deep)
+    far[1]()
     wait_all(near_rows)
     landed(0, 3, 1, 1)
     wait_all(vec_rows)
@@ -617,7 +618,7 @@
 
     grams = 0.5 * (put(acc[0:K, K:], 0) + put(acc[K:, 0:K], 0)) + put(acc[K:, K:], K)
     rows = pack(grams, 2 * K) + pack(column(column(zero16, 0, w_s), 1, b_s), 8)
-    rows = all_reduce(three_phases(0, 5), rows, (between_a, far[1], between_c))
+    rows = all_reduce(three_phases(0, 5), rows, (between_a, None, between_c))
     grams = unpack(rows[0:4], 2 * K)
     starts = unpack(rows[4:5], 8)
 
@@ -636,15 +637,24 @@
     inverse = at_zero(aug, K)
     g1, g2 = at_zero(grams, 0), at_zero(grams, K)
 
+    def as_row(col):
+        return jnp.sum(jnp.where(lane16 == sub16, col, 0.0), axis=0, keepdims=True)
+
+    def row_times(mat, row):
+        return jnp.sum(mat * row, axis=1, keepdims=True)
+
+    def times_column(mat, col):
+        return jnp.sum(mat * col, axis=0, keepdims=True)
+
     def apply(mat, col):
-        row = jnp.sum(jnp.where(lane16 == sub16, col, 0.0), axis=0, keepdims=True)
-        return jnp.sum(mat * row, axis=1, keepdims=True)
+        return row_times(mat, as_row(col))
 
     def dot(a, b):
         return jnp.sum(a * b, axis=0, keepdims=True)
 
-    coarse = coarse + apply(inverse, starts[:, 0:1] - apply(g1, coarse))
-    mu0 = apply(inverse, starts[:, 1:2] - apply(g2, coarse))
+    w_row, b_row = as_row(starts[:, 0:1]), as_row(starts[:, 1:2])
+    coarse = coarse + row_times(inverse, w_row - times_column(g1, coarse))
+    mu0 = row_times(inverse, b_row - times_column(g2, coarse))
 
 
     def residual_row(e, carry):
@@ -656,8 +666,8 @@
 
     lax.fori_loop(1, ROWS - 1, residual_row, 0, unroll=2)
     send_phase(g3_phases[1], wait_phase(g3_phases[0]))
-    for i in range(3):
-        res[i + 1] = operate(res[i])
+    for i, base in enumerate((4, 1, 2)):
+        res[i + 1] = operate(res[i]) - SHIFT * res[base]
 
     def moment_row(y, carry):
         b1, b2 = img1[y + DEPTH, :, 0:NX], img2[y]
@@ -704,7 +714,10 @@
         t[2],
         t[3] - dot(mu1, e[0]),
         t[4] - 2.0 * dot(mu1, e[1]) + dot(mu1, g2_1),
-        t[5] - 2.0 * dot(mu1, e[2]) + dot(mu1, g3_1) - dot(mu2, defl2),
+        t[5]
+        - 2.0 * dot(mu1, e[2] - SHIFT * e[1])
+        + dot(mu1, g3_1 - SHIFT * g2_1)
+        - dot(mu2, defl2),
     ]
 
     def form(poly, shift):
@@ -722,7 +735,7 @@
     curv = prev_norm = one
     for turn in range(3):
         norm = form(r_poly, 0)
-        r_image = form(r_poly, 1)
+        r_image = form(r_poly, 1) + SHIFT * norm
         if turn == 0:
             y_poly = list(r_poly)
             curv = r_image
@@ -733,27 +746,30 @@
         step_len = norm / curv
         for i, a in enumerate(y_poly):
             zeta[i] = zeta[i] + step_len * a
-        r_poly = [
-            a - step_len * b for a, b in zip(r_poly + [zero], [zero] + list(y_poly))
-        ]
+        y_image = [a + SHIFT * b for a, b in zip([zero] + y_poly, y_poly + [zero])]
+        r_poly = [a - step_len * b for a, b in zip(r_poly + [zero], y_image)]
         prev_norm = norm
 
     along_w = zeta[1] * mu1 + zeta[2] * mu2
     along_b = zeta[2] * mu1
+    res_b = (r_poly[2] - SHIFT * r_poly[3]) * mu1 + r_poly[3] * mu2
+    res_bb = r_poly[3] * mu1
 
     def final_row(y, carry):
         w, b1, b2 = vec[y + DEPTH, :, 0:NX], img1[y + DEPTH, :, 0:NX], img2[y]
         at = pl.ds(y, 1)
         comb[0, at, :] = jnp.sum(along_w * w + along_b * b1, axis=0, keepdims=True)
-        comb[1, at, :] = jnp.sum(along_w * b1 + along_b * b2, axis=0, keepdims=True)
+        comb[1, at, :] = jnp.sum(res_b * b1 + res_bb * b2, axis=0, keepdims=True)
         return carry
 
     lax.fori_loop(0, NY, final_row, 0, unroll=4)
     p0, v1, a1, a2, r0 = (res[i, 8:24, 0:NX] for i in range(5))
-    x_out[...] = (
+    out[0] = (
         st[8:24, 0:NX] + (zeta[0] * p0 + zeta[1] * v1 + zeta[2] * a1) - comb[0]
     )
-    r_out[...] = r0 - (zeta[0] * v1 + zeta[1] * a1 + zeta[2] * a2) + comb[1]
+    out[1] = (
+        r_poly[0] * r0 + (r_poly[1] * v1 + r_poly[2] * a1 + r_poly[3] * a2) - comb[1]
+    )
 
 
 def shards(right_side, first_guess, cell_mask, cond_east, cond_north, surface, recycled):
@@ -761,14 +777,13 @@
     ny_dev, nzh, nx_dev, nzl, ncore = sizes
     na, nb, nc = nx_dev * ncore, ny_dev, nzh * nzl
     nd, ne = nx_dev * ny_dev, nzh * nzl * ncore
-    field = jax.ShapeDtypeStruct((NY, NX), f32)
     vmem = pltpu.VMEM
     dma = pltpu.SemaphoreType.DMA
-    return pl.pallas_call(
+    both = pl.pallas_call(
         functools.partial(kernel, sizes),
-        out_shape=(field, field),
+        out_shape=jax.ShapeDtypeStruct((2, NY, NX), f32),
         in_specs=[pl.BlockSpec(memory_space=pl.ANY)] * 7,
-        out_specs=(pl.BlockSpec(memory_space=pltpu.VMEM),) * 2,
+        out_specs=pl.BlockSpec(memory_space=pltpu.VMEM),
         scratch_shapes=[
             vmem((ROWS, K, WIDE), f32),
             vmem((ROWS, K, WIDE), f32),
@@ -807,6 +822,7 @@
         ],
         compiler_params=pltpu.CompilerParams(collective_id=0, has_side_effects=True),
     )(right_side, first_guess, cell_mask, cond_east, cond_north, surface, recycled)
+    return both[0], both[1]
 
 
 def finer_mesh(mesh):

time: 69.5 us -> 66.5 us (0.957)
  Pallas kernels: 66.6 us -> 64.1 us
    pallas_call x1, Pallas kernels: 66.6 us -> 64.1 us  [shards(): pl.pallas_call(functools.partial(kernel, sizes), out_shape=jax.ShapeDtype...]
    unnamed x4 -> x0, local copies, waits for them, and re-layouts: 2.03 us -> none
    squeeze x0 -> x1, local copies, waits for them, and re-layouts: none -> 1.43 us  [shards(): return (both[0], both[1])]
where the time goes in v4:
time: 66.5 us; the launch traced here: 66.2 us
  Pallas kernels  64.1 us (96%)
  local copies, waits for them, and re-layouts  1.43 us (2%)
    pallas_call x1, Pallas kernels, shards(): pl.pallas_call(functools.partial(kernel, sizes), out_shape=jax.ShapeDtype...  64.1 us
    squeeze x1, local copies, waits for them, and re-layouts, shards(): return (both[0], both[1])  1.43 us

profile of v4, /device:TPU:1, one launch (start us, length us, event | category | flops | bytes accessed | tf_op | source)
XLA Modules:
  0.0 66.2 jit_solution(17985116844278407404)
XLA Ops:
  0.6 64.1 %shard_map.86 = f32[2,16,640]{2,1,0:T(8,128)} custom-call(f32[16,640]{1,0:T(8,128)} %rhs_hbm.1, f32[16,640]{1,0:T(8,128)} %guess_hbm.1, s32[16,640]{1,0:T(8,128)} %mask_hbm.1, f32[16,640]{1,0:T(8,128)} %east_hbm.1, f32[16,640]{1,0:T(8,128)} %north_hbm.1, f32[16,640]{1,0:T(8,128)} %surf_hbm.1, f32[16,16,640]{2,1,0:T(8,128)} %rec_hbm.1), custom_call_target="tpu_custom_call" | custom-call | tf_op jit(solution)/shard_map/pallas_call | solution.py:782
  64.8 1.4 %slice_bitcast_fusion = (f32[16,640]{1,0:T(8,128)}, f32[16,640]{1,0:T(8,128)}) fusion(f32[2,16,640]{2,1,0:T(8,128)} %shard_map.86), kind=kLoop, calls=%fused_computation | loop fusion | bytes 163840 | tf_op jit(solution)/shard_map/squeeze | solution.py:825

commit v5 on v4

--- a/solution.py
+++ b/solution.py
@@ -129,14 +129,6 @@
     east_of, west_of = at_cell(0, 1), at_cell(0, -1)
     corners = (at_cell(1, 1), at_cell(1, -1), at_cell(-1, 1), at_cell(-1, -1))
 
-    barrier = pltpu.get_barrier_semaphore()
-    peers = [north_of, south_of, *corners, east_of, west_of]
-    for n, me, at in ((ne, my_e, at_e), (nd, my_d, at_d), (na, my_a, at_a)):
-        for d in far_first(n):
-            peers.append(at(lax.rem(me + d, n)))
-    for peer in peers:
-        pl.semaphore_signal(barrier, inc=1, device_id=peer, device_id_type=MESH)
-
     plain = (
         (east_hbm, EAST),
         (north_hbm, NORTH),
@@ -159,6 +151,17 @@
         )
     for load in loads:
         load.start()
+
+    barrier = pltpu.get_barrier_semaphore()
+    peers = [north_of, south_of, *corners, east_of, west_of]
+    groups = [
+        [at(lax.rem(me + d, n)) for d in far_first(n)]
+        for n, me, at in ((ne, my_e, at_e), (nd, my_d, at_d), (na, my_a, at_a))
+    ]
+    for i in range(max(len(group) for group in groups)):
+        peers += [group[i] for group in groups if i < len(group)]
+    for peer in peers:
+        pl.semaphore_signal(barrier, inc=1, device_id=peer, device_id_type=MESH)
 
     nat[:, 0:8, :] = jnp.zeros((6, 8, WIDE), f32)
     nat[:, 24:32, :] = jnp.zeros((6, 8, WIDE), f32)
@@ -390,6 +393,7 @@
     start_all(vec_columns)
     start_all(near_rows)
     start_all(vec_rows)
+    far[0]()
 
     def east(v):
         return pltpu.roll(v, WIDE - 1, 1)
@@ -467,7 +471,6 @@
     start_residual()
     wait_all(vec_columns)
     unpack_vectors(DEPTH, NY, 0, 0)
-    far[0]()
     carry = (jnp.zeros((2 * K, 2 * K), f32), zero16, zero16)
     carry = lax.fori_loop(
         0, NY // 2 - 1, lambda i, c: first_pair((2 * i + 1, 2 * i + 2), c), carry
@@ -630,9 +633,16 @@
     aug = jnp.where(lane16 < K, grams, 0.0)
     aug = jnp.where(lane16 == sub16 + K, 1.0, aug)
     aug = jnp.where(lane16 == 2 * K, starts[:, 0:1], aug)
+    pivots = jnp.broadcast_to(aug[:, 0:1], (K, 128))
     for i in range(K):
-        pivot_row = aug[i : i + 1, :] / aug[i : i + 1, i : i + 1]
-        aug = jnp.where(sub16 == i, pivot_row, aug - aug[:, i : i + 1] * pivot_row)
+        scale = 1.0 / pivots[i : i + 1, :]
+        pivot_row = aug[i : i + 1, :] * scale
+        column_now = pivots
+        if i + 1 < K:
+            coming = jnp.broadcast_to(aug[:, i + 1 : i + 2], (K, 128))
+            coming_row = coming[i : i + 1, :] * scale
+            pivots = jnp.where(sub16 == i, coming_row, coming - column_now * coming_row)
+        aug = jnp.where(sub16 == i, pivot_row, aug - column_now * pivot_row)
     coarse = aug[:, 2 * K : 2 * K + 1]
     inverse = at_zero(aug, K)
     g1, g2 = at_zero(grams, 0), at_zero(grams, K)
@@ -664,7 +674,7 @@
         res[0, at, :] = r - jnp.sum(mu0 * vec[e], axis=0, keepdims=True)
         return carry
 
-    lax.fori_loop(1, ROWS - 1, residual_row, 0, unroll=2)
+    lax.fori_loop(1, ROWS - 1, residual_row, 0, unroll=11)
     send_phase(g3_phases[1], wait_phase(g3_phases[0]))
     for i, base in enumerate((4, 1, 2)):
         res[i + 1] = operate(res[i]) - SHIFT * res[base]
@@ -675,7 +685,7 @@
         terms = (b1 * v1, b1 * a1, b2 * a1)
         return tuple(total + fold(term) for total, term in zip(carry, terms))
 
-    defl = lax.fori_loop(0, NY, moment_row, (zero16,) * 3, unroll=2)
+    defl = lax.fori_loop(0, NY, moment_row, (zero16,) * 3, unroll=4)
     payload = zero16
     for i, total in enumerate(defl):
         payload = column(payload, i, total)
@@ -762,7 +772,7 @@
         comb[1, at, :] = jnp.sum(res_b * b1 + res_bb * b2, axis=0, keepdims=True)
         return carry
 
-    lax.fori_loop(0, NY, final_row, 0, unroll=4)
+    lax.fori_loop(0, NY, final_row, 0, unroll=8)
     p0, v1, a1, a2, r0 = (res[i, 8:24, 0:NX] for i in range(5))
     out[0] = (
         st[8:24, 0:NX] + (zeta[0] * p0 + zeta[1] * v1 + zeta[2] * a1) - comb[0]

time: 66.5 us -> 65.5 us (0.985)
  Pallas kernels: 64.1 us -> 63.2 us
    pallas_call x1, Pallas kernels: 64.1 us -> 63.2 us  [shards(): pl.pallas_call(functools.partial(kernel, sizes), out_shape=jax.ShapeDtype...]
where the time goes in v5:
time: 65.5 us; the launch traced here: 65.3 us
  Pallas kernels  63.2 us (96%)
  local copies, waits for them, and re-layouts  1.43 us (2%)
    pallas_call x1, Pallas kernels, shards(): pl.pallas_call(functools.partial(kernel, sizes), out_shape=jax.ShapeDtype...  63.2 us
    squeeze x1, local copies, waits for them, and re-layouts, shards(): return (both[0], both[1])  1.43 us

profile of v5, /device:TPU:1, one launch (start us, length us, event | category | flops | bytes accessed | tf_op | source)
XLA Modules:
  0.0 65.3 jit_solution(8961666727722635986)
XLA Ops:
  0.6 63.2 %shard_map.86 = f32[2,16,640]{2,1,0:T(8,128)} custom-call(f32[16,640]{1,0:T(8,128)} %rhs_hbm.1, f32[16,640]{1,0:T(8,128)} %guess_hbm.1, s32[16,640]{1,0:T(8,128)} %mask_hbm.1, f32[16,640]{1,0:T(8,128)} %east_hbm.1, f32[16,640]{1,0:T(8,128)} %north_hbm.1, f32[16,640]{1,0:T(8,128)} %surf_hbm.1, f32[16,16,640]{2,1,0:T(8,128)} %rec_hbm.1), custom_call_target="tpu_custom_call" | custom-call | tf_op jit(solution)/shard_map/pallas_call | solution.py:792
  63.9 1.4 %slice_bitcast_fusion = (f32[16,640]{1,0:T(8,128)}, f32[16,640]{1,0:T(8,128)}) fusion(f32[2,16,640]{2,1,0:T(8,128)} %shard_map.86), kind=kLoop, calls=%fused_computation | loop fusion | bytes 163840 | tf_op jit(solution)/shard_map/squeeze | solution.py:835

commit v6 on v5

--- a/solution.py
+++ b/solution.py
@@ -479,9 +479,9 @@
     far[1]()
     wait_all(near_rows)
     landed(0, 3, 1, 1)
-    wait_all(vec_rows)
     coefficients()
     start_residual()
+    wait_all(vec_rows)
     acc, w_s, b_s = first_pair((0, NY - 1), carry)
 
     def put(block, lane):
@@ -539,7 +539,7 @@
 
     def wait_phase(phase):
         send, buf, ssem, rsem, n, me, at, count = phase
-        for d in range(1, n):
+        for d in reversed(far_first(n)):
             peer = lax.rem(me + d, n)
             if count == 1:
                 src, dst = send.at[pl.ds(0, 1)], buf.at[pl.ds(peer, 1)]
@@ -552,13 +552,26 @@
                 recv_sem=rsem.at[peer],
                 device_id=at(peer),
                 device_id_type=MESH,
-            ).wait()
+            ).wait_recv()
         if count == 1:
             return jnp.sum(buf[...], axis=0, keepdims=True)
         total = buf[0]
         for i in range(1, n):
             total = total + buf[i]
         return [total[i : i + 1, :] for i in range(count)]
+
+    def finish_sends(phase):
+        send, buf, ssem, rsem, n, me, at, count = phase
+        src = send.at[pl.ds(0, count)]
+        for d in range(1, n):
+            pltpu.make_async_remote_copy(
+                src_ref=src,
+                dst_ref=src,
+                send_sem=ssem.at[d],
+                recv_sem=rsem.at[me],
+                device_id=at(lax.rem(me + d, n)),
+                device_id_type=MESH,
+            ).wait_send()
 
     def three_phases(turn, count):
         return (
@@ -580,6 +593,7 @@
             value = wait_phase(phase)
         return value
 
+    first_phases = three_phases(0, 5)
     g3_phases = three_phases(1, 2)
     kept = {}
 
@@ -618,10 +632,12 @@
         lax.fori_loop(0, DEPTH, outer_row, 0)
         acc = second_pair((0, NY - 1), kept["g3"])
         send_phase(g3_phases[0], pack(put(acc, 0), K))
+        finish_sends(first_phases[0])
+        finish_sends(first_phases[1])
 
     grams = 0.5 * (put(acc[0:K, K:], 0) + put(acc[K:, 0:K], 0)) + put(acc[K:, K:], K)
     rows = pack(grams, 2 * K) + pack(column(column(zero16, 0, w_s), 1, b_s), 8)
-    rows = all_reduce(three_phases(0, 5), rows, (between_a, None, between_c))
+    rows = all_reduce(first_phases, rows, (between_a, None, between_c))
     grams = unpack(rows[0:4], 2 * K)
     starts = unpack(rows[4:5], 8)
 
@@ -704,9 +720,13 @@
 
         lax.fori_loop(0, NY, row, 0, unroll=4)
         send_phase(g3_phases[2], wait_phase(g3_phases[1]))
+        for phase in (first_phases[2], g3_phases[0], g3_phases[1]):
+            finish_sends(phase)
 
     def last_gram():
         kept["g3"] = unpack(wait_phase(g3_phases[2]), K)
+        for phase in (g3_phases[2], *two_phases):
+            finish_sends(phase)
 
     row = all_reduce(two_phases, pack(payload, 8)[0], (before_scalars, last_gram))
     sums = unpack([row], 8)

time: 65.5 us -> 65.3 us (level)
  no operation moved by 1% of the time
where the time goes in v6:
time: 65.3 us; the launch traced here: 65.1 us
  Pallas kernels  63 us (96%)
  local copies, waits for them, and re-layouts  1.43 us (2%)
    pallas_call x1, Pallas kernels, shards(): pl.pallas_call(functools.partial(kernel, sizes), out_shape=jax.ShapeDtype...  63 us
    squeeze x1, local copies, waits for them, and re-layouts, shards(): return (both[0], both[1])  1.43 us

profile of v6, /device:TPU:1, one launch (start us, length us, event | category | flops | bytes accessed | tf_op | source)
XLA Modules:
  0.0 65.1 jit_solution(1120372377679079913)
XLA Ops:
  0.6 63.0 %shard_map.86 = f32[2,16,640]{2,1,0:T(8,128)} custom-call(f32[16,640]{1,0:T(8,128)} %rhs_hbm.1, f32[16,640]{1,0:T(8,128)} %guess_hbm.1, s32[16,640]{1,0:T(8,128)} %mask_hbm.1, f32[16,640]{1,0:T(8,128)} %east_hbm.1, f32[16,640]{1,0:T(8,128)} %north_hbm.1, f32[16,640]{1,0:T(8,128)} %surf_hbm.1, f32[16,16,640]{2,1,0:T(8,128)} %rec_hbm.1), custom_call_target="tpu_custom_call" | custom-call | tf_op jit(solution)/shard_map/pallas_call | solution.py:812
  63.7 1.4 %slice_bitcast_fusion = (f32[16,640]{1,0:T(8,128)}, f32[16,640]{1,0:T(8,128)}) fusion(f32[2,16,640]{2,1,0:T(8,128)} %shard_map.86), kind=kLoop, calls=%fused_computation | loop fusion | bytes 163840 | tf_op jit(solution)/shard_map/squeeze | solution.py:855

commit v7 on v6

--- a/solution.py
+++ b/solution.py
@@ -488,11 +488,16 @@
         wide = jnp.concatenate([block, jnp.zeros((K, 128 - block.shape[1]), f32)], axis=1)
         return pltpu.roll(wide, lane, 1) if lane else wide
 
+    lane8 = lax.rem(lane16, 8)
+
     def column(payload, lane, total):
-        return jnp.where(lane16 == lane, jnp.sum(total, axis=1, keepdims=True), payload)
+        return jnp.where(lane8 == lane, jnp.sum(total, axis=1, keepdims=True), payload)
+
+    def pick(row, lane):
+        return jnp.sum(jnp.where(lane16 == 8 * sub16 + lane, row, 0.0), axis=1, keepdims=True)
 
     def pack(v, width):
-        per, shift = 128 // width, width
+        per, shift = 128 // width, 128 if width == 8 else width
         while shift < 128:
             v = v + pltpu.roll(v, shift, 1)
             shift *= 2
@@ -639,7 +644,7 @@
     rows = pack(grams, 2 * K) + pack(column(column(zero16, 0, w_s), 1, b_s), 8)
     rows = all_reduce(first_phases, rows, (between_a, None, between_c))
     grams = unpack(rows[0:4], 2 * K)
-    starts = unpack(rows[4:5], 8)
+    starts = [pick(rows[4], lane) for lane in (0, 1)]
 
 
     def at_zero(v, lane):
@@ -648,7 +653,7 @@
 
     aug = jnp.where(lane16 < K, grams, 0.0)
     aug = jnp.where(lane16 == sub16 + K, 1.0, aug)
-    aug = jnp.where(lane16 == 2 * K, starts[:, 0:1], aug)
+    aug = jnp.where(lane16 == 2 * K, starts[0], aug)
     pivots = jnp.broadcast_to(aug[:, 0:1], (K, 128))
     for i in range(K):
         scale = 1.0 / pivots[i : i + 1, :]
@@ -678,7 +683,7 @@
     def dot(a, b):
         return jnp.sum(a * b, axis=0, keepdims=True)
 
-    w_row, b_row = as_row(starts[:, 0:1]), as_row(starts[:, 1:2])
+    w_row, b_row = as_row(starts[0]), as_row(starts[1])
     coarse = coarse + row_times(inverse, w_row - times_column(g1, coarse))
     mu0 = row_times(inverse, b_row - times_column(g2, coarse))
 
@@ -709,7 +714,7 @@
     for i, (a, b) in enumerate(((0, 0), (0, 1), (1, 1), (1, 2), (2, 2), (2, 3))):
         total = jnp.sum(fold(inner[a] * inner[b]), axis=0, keepdims=True)
         total = jnp.sum(total, axis=1, keepdims=True)
-        payload = jnp.where((lane16 == 3) & (sub16 == i), total, payload)
+        payload = jnp.where((lane8 == 3) & (sub16 == i), total, payload)
 
     def before_scalars():
         def row(y, carry):
@@ -729,11 +734,11 @@
             finish_sends(phase)
 
     row = all_reduce(two_phases, pack(payload, 8)[0], (before_scalars, last_gram))
-    sums = unpack([row], 8)
 
     g3 = kept["g3"]
-    e = [sums[:, i : i + 1] for i in range(3)]
-    t = [sums[i : i + 1, 3:4] for i in range(6)]
+    e = [pick(row, i) for i in range(3)]
+    t_all = pick(row, 3)
+    t = [t_all[i : i + 1, :] for i in range(6)]
     mu1 = apply(inverse, e[0])
     g2_1, g3_1 = apply(g2, mu1), apply(g3, mu1)
     defl2 = e[1] - g2_1

time: 65.3 us -> 64.4 us (0.986)
  Pallas kernels: 63 us -> 62.1 us
    pallas_call x1, Pallas kernels: 63 us -> 62.1 us  [shards(): pl.pallas_call(functools.partial(kernel, sizes), out_shape=jax.ShapeDtype...]
where the time goes in v7:
time: 64.4 us; the launch traced here: 64.2 us
  Pallas kernels  62.1 us (96%)
  local copies, waits for them, and re-layouts  1.43 us (2%)
    pallas_call x1, Pallas kernels, shards(): pl.pallas_call(functools.partial(kernel, sizes), out_shape=jax.ShapeDtype...  62.1 us
    squeeze x1, local copies, waits for them, and re-layouts, shards(): return (both[0], both[1])  1.43 us

profile of v7, /device:TPU:1, one launch (start us, length us, event | category | flops | bytes accessed | tf_op | source)
XLA Modules:
  0.0 64.2 jit_solution(13817149144036024802)
XLA Ops:
  0.6 62.1 %shard_map.86 = f32[2,16,640]{2,1,0:T(8,128)} custom-call(f32[16,640]{1,0:T(8,128)} %rhs_hbm.1, f32[16,640]{1,0:T(8,128)} %guess_hbm.1, s32[16,640]{1,0:T(8,128)} %mask_hbm.1, f32[16,640]{1,0:T(8,128)} %east_hbm.1, f32[16,640]{1,0:T(8,128)} %north_hbm.1, f32[16,640]{1,0:T(8,128)} %surf_hbm.1, f32[16,16,640]{2,1,0:T(8,128)} %rec_hbm.1), custom_call_target="tpu_custom_call" | custom-call | tf_op jit(solution)/shard_map/pallas_call | solution.py:817
  62.8 1.4 %slice_bitcast_fusion = (f32[16,640]{1,0:T(8,128)}, f32[16,640]{1,0:T(8,128)}) fusion(f32[2,16,640]{2,1,0:T(8,128)} %shard_map.86), kind=kLoop, calls=%fused_computation | loop fusion | bytes 163840 | tf_op jit(solution)/shard_map/squeeze | solution.py:860

commit v8 on v7

--- a/solution.py
+++ b/solution.py
@@ -706,7 +706,7 @@
         terms = (b1 * v1, b1 * a1, b2 * a1)
         return tuple(total + fold(term) for total, term in zip(carry, terms))
 
-    defl = lax.fori_loop(0, NY, moment_row, (zero16,) * 3, unroll=4)
+    defl = lax.fori_loop(0, NY, moment_row, (zero16,) * 3, unroll=8)
     payload = zero16
     for i, total in enumerate(defl):
         payload = column(payload, i, total)
@@ -797,7 +797,7 @@
         comb[1, at, :] = jnp.sum(res_b * b1 + res_bb * b2, axis=0, keepdims=True)
         return carry
 
-    lax.fori_loop(0, NY, final_row, 0, unroll=8)
+    lax.fori_loop(0, NY, final_row, 0, unroll=16)
     p0, v1, a1, a2, r0 = (res[i, 8:24, 0:NX] for i in range(5))
     out[0] = (
         st[8:24, 0:NX] + (zeta[0] * p0 + zeta[1] * v1 + zeta[2] * a1) - comb[0]

time: 64.4 us -> 64.3 us (level)
  no operation moved by 1% of the time
where the time goes in v8:
time: 64.3 us; the launch traced here: 64.1 us
  Pallas kernels  62 us (96%)
  local copies, waits for them, and re-layouts  1.43 us (2%)
    pallas_call x1, Pallas kernels, shards(): pl.pallas_call(functools.partial(kernel, sizes), out_shape=jax.ShapeDtype...  62 us
    squeeze x1, local copies, waits for them, and re-layouts, shards(): return (both[0], both[1])  1.43 us

profile of v8, /device:TPU:1, one launch (start us, length us, event | category | flops | bytes accessed | tf_op | source)
XLA Modules:
  0.0 64.1 jit_solution(1149414360901943179)
XLA Ops:
  0.6 62.0 %shard_map.86 = f32[2,16,640]{2,1,0:T(8,128)} custom-call(f32[16,640]{1,0:T(8,128)} %rhs_hbm.1, f32[16,640]{1,0:T(8,128)} %guess_hbm.1, s32[16,640]{1,0:T(8,128)} %mask_hbm.1, f32[16,640]{1,0:T(8,128)} %east_hbm.1, f32[16,640]{1,0:T(8,128)} %north_hbm.1, f32[16,640]{1,0:T(8,128)} %surf_hbm.1, f32[16,16,640]{2,1,0:T(8,128)} %rec_hbm.1), custom_call_target="tpu_custom_call" | custom-call | tf_op jit(solution)/shard_map/pallas_call | solution.py:817
  62.6 1.4 %slice_bitcast_fusion = (f32[16,640]{1,0:T(8,128)}, f32[16,640]{1,0:T(8,128)}) fusion(f32[2,16,640]{2,1,0:T(8,128)} %shard_map.86), kind=kLoop, calls=%fused_computation | loop fusion | bytes 163840 | tf_op jit(solution)/shard_map/squeeze | solution.py:860
